TPU v7x, 256 devices: a whole 4x4x8 slice. The times are simulated.
256 devices in a mesh: px: 32 (over x, y, core), py: 8 (over z).
Axes of the slice: x: 4, y: 4, z: 8, core: 2. Of those that a mesh axis runs over, the one named last changes fastest.
Arguments:
- cell_ids: int32 [32, 5120, 128], P('px', 'py'), may hold values from 0 to 32767, as said below
- offset_x: bfloat16 [32, 5120, 128], P('px', 'py'), may hold values from 0 to 1
- offset_y: bfloat16 [32, 5120, 128], P('px', 'py'), may hold values from 0 to 1
- mass: bfloat16 [32, 5120, 128], P('px', 'py'), may hold values from 0.25 to 4
- live: int32 [32, 5120, 128], P('px', 'py'), may hold values from 0 to 1, as said below
- tile_owner: int32 [32, 5120], P('px', 'py'), may hold values from 0 to 31, as said below
- counts: int32 [32, 8, 256], P('px', 'py'), may hold values from 0 to 7680, as said below
Outputs:
- spectrum: float32 [2, 8, 1024, 1024], P(None, None, ('px', 'py'))
- bucket_start: int32 [32, 8, 256], P('px', 'py')
Inputs may be any that keep to these rules, and one draw needn't show every extreme that they name: A device's tiles stand in order of bucket, bucket = tile_owner * 8 + plane. One device has at most 60 tiles of one owner; in every draw, in each column of py, one owner has exactly 60 tiles on every device of that column. `cell_ids`: cell = (plane * 32 + row) * 128 + column, with row inside the owner's block of rows and column inside the device's block of columns; all slots of a tile, padded ones too, carry the tile's plane. In a tile the live particles come first; only the last tile of a bucket on a device has padded slots. counts[i, j, b] is the number of live particles in the tiles of bucket b on device (i, j); in every draw some bucket of every device holds 7680.
All inputs are finite; a program needn't handle non-finite values.
Results may differ from a plain program's by a relative error of at most 0.0003.
The roundings to bfloat16 on the way count: a program that leaves them out, or rounds other values in their place, can miss the bound.
Values may be sent and summed in bfloat16 or wider, within the bound.
A program may use at most 128 MiB of HBM per device.

v0:
```python
import math

import jax
import jax.numpy as jnp
from jax import lax
from jax.sharding import Mesh
from jax.sharding import PartitionSpec as P

NX = 1024
NY = 1024
PLANES = 8
PX = ("px_0", "px_1", "px_2")
PX_PY = ("px_0", "px_1", "px_2", "py")


BETA = 18.4


def passed_along(value, axis, steps):
    count = lax.axis_size(axis)
    pairs = [(source, (source + steps) % count) for source in range(count)]
    return lax.ppermute(value, axis, pairs)


def over_axes(value, axes):
    for axis in axes:
        value = lax.psum(value, axis)
    return value


def in_blocks(value, dim, devices):
    before, after = (value.shape[:dim], value.shape[dim + 1 :])
    return jnp.moveaxis(value.reshape(*before, devices, -1, *after), dim, 0)


def laid_out(parts, dim):
    lengths = list(parts.shape[1:])
    lengths[dim] *= parts.shape[0]
    return jnp.moveaxis(parts, 0, dim).reshape(lengths)


def one_exchange(value, axis, axes, splits, concats):
    sizes = [lax.axis_size(a) for a in axes]
    parts = in_blocks(value, splits[0], sizes[0])
    parts = jnp.moveaxis(in_blocks(parts, splits[1] + 1, sizes[1]), 0, 1)
    inside = parts.shape[2:]
    parts = parts.reshape(-1, *inside)
    parts = lax.all_to_all(parts, axis, split_axis=0, concat_axis=0, tiled=True)
    parts = laid_out(parts.reshape(*sizes, *inside), concats[0] + 1)
    return laid_out(parts, concats[1])


def from_everyone(value, axis):
    devices = lax.axis_size(axis)
    return lax.all_to_all(
        jnp.broadcast_to(value[None], (devices, *value.shape)), axis, 0, 0, tiled=True
    )


def folded_in_pairs(pieces, combine):
    while len(jax.tree.leaves(pieces)[0]) > 1:
        pieces = jax.vmap(combine)(*(pieces[side::2] for side in (0, 1)))
    return pieces[0]


def carried_in(value, axis, combine, identity):
    devices, index = (lax.axis_size(axis), lax.axis_index(axis))
    passed = jnp.arange(devices) < index

    def kept(part, zero, own):
        part = jnp.where(
            passed.reshape(-1, *(1 for _ in own.shape)), part, jnp.asarray(zero, own.dtype)
        )
        return part

    pieces = from_everyone(value, axis)
    return folded_in_pairs(kept(pieces, identity, value), combine)


def of_everyone(value, axis):
    everything = from_everyone(value, axis)
    return jnp.sum(everything, axis=0)


def window_weights(local_index, fraction, extent, scaling):
    tap_steps = jnp.arange(-3, 5, dtype=jnp.int32)
    position = (
        tap_steps.astype(jnp.float32)[None, None, :] - fraction.astype(jnp.float32)[:, :, None]
    ) / 4.0
    taps = jnp.exp(BETA * (jnp.sqrt(1.0 - position * position) - 1.0))
    if scaling is not None:
        taps = taps * scaling[:, :, None]
    taps = taps.astype(jnp.bfloat16)
    spot_index = jnp.arange(extent, dtype=jnp.int32)
    offset_step = spot_index[None, None, :] - 4 - local_index[:, :, None]
    placed = jnp.zeros(offset_step.shape, jnp.bfloat16)
    for step_number in range(8):
        placed = jnp.where(
            offset_step == step_number - 3, taps[:, :, step_number : step_number + 1], placed
        )
    return placed


def spread_tiles(tile_cells, frac_x, frac_y, masses, slot_ids, slot_count, row_count, col_count):
    tile_total = tile_cells.shape[0]
    turn_count = max(1, tile_total // 256)
    while tile_total % turn_count != 0:
        turn_count = turn_count - 1
    block_size = tile_total // turn_count

    def add_block(running, pieces):
        block_cells, block_x, block_y, block_mass, block_slot = pieces
        local_y = block_cells % col_count
        local_x = block_cells // col_count % row_count
        weight_x = window_weights(local_x, block_x, row_count + 8, None)
        weight_y = window_weights(local_y, block_y, col_count + 8, block_mass.astype(jnp.float32))
        contrib = jnp.einsum("tna,tnb->tab", weight_x, weight_y, preferred_element_type=jnp.float32)
        return (running.at[block_slot].add(contrib), None)

    stacked = tuple(
        (
            member_array.reshape((turn_count, block_size) + member_array.shape[1:])
            for member_array in (tile_cells, frac_x, frac_y, masses, slot_ids)
        )
    )
    initial = jnp.zeros((slot_count, row_count + 8, col_count + 8), jnp.float32)
    return lax.scan(add_block, initial, stacked)[0]


def fold_rows(extended, row_count):
    core = extended[:, 4 : row_count + 4, :]
    for direction in (1, -1):
        if direction == 1:
            rim_cells = extended[:, row_count + 4 :, :]
        else:
            rim_cells = extended[:, :4, :]
        moved = passed_along(rim_cells, PX, direction)
        if direction == 1:
            core = core.at[:, :4, :].add(moved)
        else:
            core = core.at[:, row_count - 4 :, :].add(moved)
    return core


def fold_columns(extended, col_count):
    core = extended[:, :, 4 : col_count + 4]
    for direction in (1, -1):
        if direction == 1:
            rim_cells = extended[:, :, col_count + 4 :]
        else:
            rim_cells = extended[:, :, :4]
        moved = passed_along(rim_cells, "py", direction)
        if direction == 1:
            core = core.at[:, :, :4].add(moved)
        else:
            core = core.at[:, :, col_count - 4 :].add(moved)
    return core


def add_counts(earlier, later):
    return earlier + later


def project(data_block, table):
    return jnp.einsum("pqy,qk->pyk", data_block, table, precision=lax.Precision.HIGHEST)


def local(cell_ids, offset_x, offset_y, mass, live, tile_owner, counts):
    px_count = lax.axis_size(PX)
    py_count = lax.axis_size("py")
    row_count = NX // px_count
    col_count = NY // py_count
    tile_cells = cell_ids[0]
    frac_x = offset_x[0]
    frac_y = offset_y[0]
    masses = jnp.where(live[0] == 1, mass[0], jnp.zeros_like(mass[0]))
    owners = tile_owner[0]
    plane_size = row_count * col_count
    buckets = owners * PLANES + tile_cells[:, 0] // plane_size
    blocks = spread_tiles(
        tile_cells, frac_x, frac_y, masses, buckets, px_count * PLANES, row_count, col_count
    )
    blocks = blocks.reshape((px_count, PLANES) + blocks.shape[1:])
    extended = lax.psum_scatter(blocks, PX, scatter_dimension=0, tiled=True)[0]
    density = fold_columns(fold_rows(extended, row_count), col_count)
    grand_total = over_axes(jnp.sum(density), PX_PY)
    contrast = density / (grand_total / (PLANES * NX * NY)) - 1.0
    by_rows = lax.all_to_all(contrast, "py", split_axis=1, concat_axis=2, tiled=True)
    part_rows = by_rows.shape[1]
    freq_y = jnp.arange(NY, dtype=jnp.int32)
    angle_y = 2.0 * math.pi / NY * (freq_y[:, None] * freq_y[None, :] % NY).astype(jnp.float32)
    flat_rows = by_rows.reshape(-1, NY)
    real_y = jnp.dot(flat_rows, jnp.cos(angle_y), precision=lax.Precision.HIGHEST).reshape(
        by_rows.shape
    )
    imag_y = -jnp.dot(flat_rows, jnp.sin(angle_y), precision=lax.Precision.HIGHEST).reshape(
        by_rows.shape
    )
    real_cols, imag_cols = (
        one_exchange(real_y, PX_PY, (PX, "py"), (2, 2), (1, 1)),
        one_exchange(imag_y, PX_PY, (PX, "py"), (2, 2), (1, 1)),
    )
    row_order = jnp.arange(NX, dtype=jnp.int32)
    within = row_order % part_rows
    from_px = row_order // part_rows % px_count
    from_py = row_order // (part_rows * px_count)
    true_x = from_px * row_count + from_py * part_rows + within
    angle_x = 2.0 * math.pi / NX * (true_x[:, None] * row_order[None, :] % NX).astype(jnp.float32)
    cos_x = jnp.cos(angle_x)
    sin_x = jnp.sin(angle_x)
    out_real = project(real_cols, cos_x) + project(imag_cols, sin_x)
    out_imag = project(imag_cols, cos_x) - project(real_cols, sin_x)
    spectrum = jnp.stack([out_real, out_imag]) * (1.0 / math.sqrt(NX * NY))
    earlier_sum = carried_in(counts, PX, add_counts, jnp.zeros_like(counts))
    column_sum = of_everyone(counts, PX)
    preceding = jnp.cumsum(column_sum, axis=-1) - column_sum
    bucket_start = (preceding + earlier_sum).astype(jnp.int32)
    return (spectrum, bucket_start)


def solution(mesh):
    torus = Mesh(mesh.devices.reshape(4, 4, 2, mesh.shape["py"]), ("px_0", "px_1", "px_2", "py"))
    return jax.shard_map(
        local,
        mesh=torus,
        in_specs=(
            P(PX, "py", None),
            P(PX, "py", None),
            P(PX, "py", None),
            P(PX, "py", None),
            P(PX, "py", None),
            P(PX, "py"),
            P(PX, "py", None),
        ),
        out_specs=(P(None, None, PX_PY, None), P(PX, "py", None)),
        check_vma=False,
    )
```

profile of v0, /device:TPU:1, one launch (start us, length us, event | category | flops | bytes accessed | tf_op | source)
XLA Modules:
  0.0 512.6 jit_solution(7312944514820690766)
XLA Ops:
  10.4 4.6 broadcast_in_dim.291
  15.0 149.3 %while.17 = (s32[]{:T(128)}, f32[256,40,136]{2,1,0:T(8,128)}, s32[2,320]{1,0:T(2,128)S(1)}, s32[2,320,128]{2,1,0:T(8,128)S(1)}, bf16[2,320,128]{2,1,0:T(8,128)(2...) while((s32[]{:T(128)}, f32[256,40,136]{2,1,0:T(8,128)}, ...), condition=%wide.region_2.3_spmd, body=%wide.region_0.2_spmd.sunk | while | flops 576451712 | bytes 35394856 | solution.py:127
  16.9 19.7 %fusion.186 = f32[320,40,136]{2,1,0:T(8,128)} fusion(s32[320,128]{1,0:T(8,128)S(1)} %add_select_fusion.12, s32[136]{0:T(256)S(1)} %iota_add_fusion.4, bf16[320,128]{1,0:T(8,128)(2,1)S(1)} %get-tuple-element.307, bf16[320,128]{1,0:T(8,128)(2,1)S(1)} %get-tuple-element.308, bf16[320,128]{1,0:T(8,128)(2,1)S(1)} %get-tuple-element.309, ...), kind=kOutput, calls=%fused_computation.25.clone.1 | convolution fusion | flops 568197120 | bytes 8602304 | tf_op jit(solution)/shard_map/while/body/eval_jaxpr/tna,tnb->tab/dot_general | solution.py:117
  36.7 52.2 %scatter_fusion = f32[256,40,136]{2,1,0:T(8,128)} fusion(f32[256,40,136]{2,1,0:T(8,128)} %get-tuple-element.334, s32[320]{0:T(512)S(1)} %fusion.185, f32[320,40,136]{2,1,0:T(8,128)} %fusion.186), kind=kCustom, calls=%fused_computation.clone.1 | custom fusion | flops 1740800 | bytes 20890880 | tf_op jit(solution)/shard_map/while/body/eval_jaxpr/scatter-add | solution.py:118
  90.8 19.7 %fusion.186 = f32[320,40,136]{2,1,0:T(8,128)} fusion(s32[320,128]{1,0:T(8,128)S(1)} %add_select_fusion.12, s32[136]{0:T(256)S(1)} %iota_add_fusion.4, bf16[320,128]{1,0:T(8,128)(2,1)S(1)} %get-tuple-element.307, bf16[320,128]{1,0:T(8,128)(2,1)S(1)} %get-tuple-element.308, bf16[320,128]{1,0:T(8,128)(2,1)S(1)} %get-tuple-element.309, ...), kind=kOutput, calls=%fused_computation.25.clone.1 | convolution fusion | flops 568197120 | bytes 8602304 | tf_op jit(solution)/shard_map/while/body/eval_jaxpr/tna,tnb->tab/dot_general | solution.py:117
  110.5 53.7 %scatter_fusion = f32[256,40,136]{2,1,0:T(8,128)} fusion(f32[256,40,136]{2,1,0:T(8,128)} %get-tuple-element.334, s32[320]{0:T(512)S(1)} %fusion.185, f32[320,40,136]{2,1,0:T(8,128)} %fusion.186), kind=kCustom, calls=%fused_computation.clone.1 | custom fusion | flops 1740800 | bytes 20890880 | tf_op jit(solution)/shard_map/while/body/eval_jaxpr/scatter-add | solution.py:118
  165.5 9.0 %all-to-all-start.3 = ((s32[32,1,1,256]{3,2,1,0:T(1,128)}), s32[32,1,1,256]{3,2,1,0:T(1,128)S(1)}, u32[]{:S(2)}, u32[]{:S(2)}) async-start(s32[32,1,1,256]{3,2,1,0:T(1,128)} %broadcast_in_dim.294), calls=%async_computation.4 | async-start | bytes 65536 | tf_op jit(solution)/shard_map/all_to_all | solution.py:55
  174.6 17.5 %fusion.74 = f32[1024,1024]{1,0:T(8,128)} fusion(s32[1024]{0:T(1024)S(1)} %mul.196), kind=kLoop, calls=%fused_computation.133 | loop fusion | flops 14680064 | bytes 4198400 | tf_op jit(solution)/shard_map/cos | solution.py:193
  192.1 80.8 %reduce-scatter.2.cloned.1.call-done = f32[1,8,40,136]{3,2,1,0:T(8,128)} async-done(((f32[32,8,40,136]{3,2,1,0:T(8,128)}), f32[1,8,40,136]{3,2,1,0:T(8,128)}) %reduce-scatter.2.cloned.1.call-update) | async-done | bytes 174096 | tf_op jit(solution)/shard_map/reduce_scatter | solution.py:184
  273.8 3.3 collective-permute-start
  290.3 7.8 %psum.28 = f32[]{:T(128)} all-reduce(f32[]{:T(128)} %reduce_sum.20), channel_id=1, replica_groups=mesh['px_0'=4,'px_1'=4,'px_2'=2,'py'=8] {'px_0'}, use_global_device_ids=true, to_apply=%region_5.6 | all-reduce | flops 1 | bytes 8 | tf_op jit(solution)/shard_map/psum | solution.py:27
  298.1 12.9 %psum.29 = f32[]{:T(128)} all-reduce(f32[]{:T(128)} %psum.28), channel_id=1, replica_groups=mesh['px_0'=4,'px_1'=4,'px_2'=2,'py'=8] {'px_1'}, use_global_device_ids=true, to_apply=%region_6.7 | all-reduce | flops 1 | bytes 8 | tf_op jit(solution)/shard_map/psum | solution.py:27
  311.0 3.1 psum.30
  314.5 14.9 %psum.31 = f32[]{:T(128)} all-reduce(f32[]{:T(128)} %psum.30), channel_id=1, replica_groups=mesh['px_0'=4,'px_1'=4,'px_2'=2,'py'=8] {'py'}, use_global_device_ids=true, to_apply=%region_8.9 | all-reduce | flops 1 | bytes 8 | tf_op jit(solution)/shard_map/psum | solution.py:27
  330.8 5.8 %all-to-all-start = ((f32[8,32,128]{2,0,1:T(8,128)}), f32[8,32,128]{2,0,1:T(8,128)S(1)}, u32[]{:S(2)}, u32[]{:S(2)}) async-start(f32[8,32,128]{2,0,1:T(8,128)} %copy.60), calls=%async_computation.1 | async-start | bytes 262144 | tf_op jit(solution)/shard_map/all_to_all | solution.py:188
  336.9 7.6 %all-to-all-done = f32[8,32,128]{2,0,1:T(8,128)S(1)} async-done(((f32[8,32,128]{2,0,1:T(8,128)}), f32[8,32,128]{2,0,1:T(8,128)S(1)}, u32[]{:S(2)}, u32[]{:S(2)}) %all-to-all-start) | async-done | bytes 131104 | tf_op jit(solution)/shard_map/all_to_all | solution.py:188
  344.5 18.0 %fusion.125 = f32[8,4,1024]{2,0,1:T(8,128)S(1)} fusion(f32[8,4,8,128]{3,0,1,2:T(8,128)S(1)} %bitcast.201), kind=kOutput, calls=%fused_computation.171 | convolution fusion | flops 417366016 | bytes 262144 | tf_op jit(solution)/shard_map/dot_general | solution.py:196
  368.3 10.7 %all-to-all-start.2 = ((f32[256,1,128]{2,1,0:T(1,128)}), f32[256,1,128]{2,1,0:T(1,128)S(1)}, u32[]{:S(2)}, u32[]{:S(2)}) async-start(f32[256,1,128]{2,1,0:T(1,128)} %reshape.509), calls=%async_computation.3 | async-start | bytes 262144 | tf_op jit(solution)/shard_map/all_to_all | solution.py:48
  379.0 11.3 %convolution_bitcast_fusion = f32[32,8,4,32]{3,1,0,2:T(8,128)S(1)} fusion(f32[32,32,1024,1]{2,1,0,3:T(8,128)} %bitcast.187, f32[8,4,8,128]{3,0,1,2:T(8,128)S(1)} %bitcast.202), kind=kOutput, calls=%fused_computation.166 | convolution fusion | flops 402653184 | bytes 4456448 | tf_op jit(solution)/shard_map/dot_general | solution.py:193
  395.9 14.3 %all-to-all-start.1 = ((f32[256,1,128]{2,1,0:T(1,128)}), f32[256,1,128]{2,1,0:T(1,128)S(1)}, u32[]{:S(2)}, u32[]{:S(2)}) async-start(f32[256,1,128]{2,1,0:T(1,128)} %reshape.507), calls=%async_computation.2 | async-start | bytes 262144 | tf_op jit(solution)/shard_map/all_to_all | solution.py:48
  431.0 18.4 %fusion.87 = f32[8,4,1024]{2,0,1:T(8,128)S(1)} fusion(s32[1024]{0:T(1024)S(1)} %fusion.147, f32[8,8,128,4]{2,0,1,3:T(8,128)S(1)} %copy.73), kind=kOutput, calls=%fused_computation.145 | convolution fusion | flops 417333248 | bytes 266240 | tf_op jit(solution)/shard_map/pqy,qk->pyk/dot_general | solution.py:165
  449.4 18.4 %fusion.85 = f32[8,4,1024]{2,0,1:T(8,128)S(1)} fusion(s32[1024]{0:T(1024)S(1)} %fusion.147, f32[8,8,128,4]{2,0,1,3:T(8,128)S(1)} %copy.67), kind=kOutput, calls=%fused_computation.143 | convolution fusion | flops 417333248 | bytes 266240 | tf_op jit(solution)/shard_map/pqy,qk->pyk/dot_general | solution.py:165
  467.9 18.3 %fusion.116 = f32[1,8,4,1024]{3,1,2,0:T(8,128)S(1)} fusion(f32[8,4,1024]{2,0,1:T(8,128)S(1)} %fusion.87, s32[1024]{0:T(1024)S(1)} %fusion.147, f32[8,8,128,4]{2,0,1,3:T(8,128)S(1)} %copy.67), kind=kOutput, calls=%fused_computation.168 | convolution fusion | flops 417366016 | bytes 397312 | tf_op jit(solution)/shard_map/pqy,qk->pyk/dot_general | solution.py:165
  486.2 18.2 %fusion.122 = f32[1,8,4,1024]{3,1,2,0:T(8,128)S(1)} fusion(f32[8,4,1024]{2,0,1:T(8,128)S(1)} %fusion.85, s32[1024]{0:T(1024)S(1)} %fusion.147, f32[8,8,128,4]{2,0,1,3:T(8,128)S(1)} %copy.73), kind=kOutput, calls=%fused_computation.170 | convolution fusion | flops 417366016 | bytes 397312 | tf_op jit(solution)/shard_map/pqy,qk->pyk/dot_general | solution.py:165
  (95 shorter events, 56.8 us)
Async XLA Ops:
  7.2 265.8 %reduce-scatter.2.cloned.1.call-start = ((), (), s32[]{:S(2)}) async-start(), calls=%async_computation.5 | async-start | bytes 10813440 | tf_op jit(solution)/shard_map/reduce_scatter | solution.py:184
  10.3 4.6 copy-start
  10.4 4.6 copy-start.1
  10.4 4.6 copy-start.2
  164.2 0.7 copy-start.3
  165.5 118.0 %all-to-all-start.3 = ((s32[32,1,1,256]{3,2,1,0:T(1,128)}), s32[32,1,1,256]{3,2,1,0:T(1,128)S(1)}, u32[]{:S(2)}, u32[]{:S(2)}) async-start(s32[32,1,1,256]{3,2,1,0:T(1,128)} %broadcast_in_dim.294), calls=%async_computation.4 | async-start | bytes 65536 | tf_op jit(solution)/shard_map/all_to_all | solution.py:55
  273.8 4.4 collective-permute-start
  278.2 3.7 collective-permute-start.1
  282.0 5.6 %collective-permute-start.2 = (f32[8,32,4]{2,1,0:T(8,128)S(1)}, f32[8,32,4]{2,1,0:T(8,128)S(1)}, u32[]{:S(2)}, u32[]{:S(2)}) collective-permute-start(f32[8,32,4]{2,1,0:T(8,128)S(1)} %get-tuple-element.235), channel_id=1, source_target_pairs={{0,1},{1,2},{2,3},{3,4},{4,5},{5,6},{6,7},{7,0},{8,9},{9,10},{10,1... | collective-permute-start | bytes 12296 | tf_op jit(solution)/shard_map/ppermute | solution.py:22
  283.7 4.3 collective-permute-start.3
  330.8 13.7 %all-to-all-start = ((f32[8,32,128]{2,0,1:T(8,128)}), f32[8,32,128]{2,0,1:T(8,128)S(1)}, u32[]{:S(2)}, u32[]{:S(2)}) async-start(f32[8,32,128]{2,0,1:T(8,128)} %copy.60), calls=%async_computation.1 | async-start | bytes 262144 | tf_op jit(solution)/shard_map/all_to_all | solution.py:188
  368.3 27.6 %all-to-all-start.2 = ((f32[256,1,128]{2,1,0:T(1,128)}), f32[256,1,128]{2,1,0:T(1,128)S(1)}, u32[]{:S(2)}, u32[]{:S(2)}) async-start(f32[256,1,128]{2,1,0:T(1,128)} %reshape.509), calls=%async_computation.3 | async-start | bytes 262144 | tf_op jit(solution)/shard_map/all_to_all | solution.py:48
  395.9 26.8 %all-to-all-start.1 = ((f32[256,1,128]{2,1,0:T(1,128)}), f32[256,1,128]{2,1,0:T(1,128)S(1)}, u32[]{:S(2)}, u32[]{:S(2)}) async-start(f32[256,1,128]{2,1,0:T(1,128)} %reshape.507), calls=%async_computation.2 | async-start | bytes 262144 | tf_op jit(solution)/shard_map/all_to_all | solution.py:48
Sparse Core Ops, SparseCore 0:
  164.4 108.5 reduce-scatter.1
where the time goes:
time: 523 us; the launch traced here: 513 us
  matrix products  142 us (27%)
  other arithmetic  134 us (26%)
  waiting for transfers between devices  96.3 us (18%)
  starting transfers between devices  46.5 us (9%)
  local copies, waits for them, and re-layouts  39.8 us (8%)
  blocking collectives  38.8 us (7%)
  between operations  15.4 us (3%)
    scatter-add x2, other arithmetic, add_block(): return (running.at[block_slot].add(contrib), None)  106 us
    reduce_scatter x1, waiting for transfers between devices, local(): extended = lax.psum_scatter(blocks, PX, scatter_dimension=0, tiled=True)[0]  80.8 us
    dot_general x4, matrix products, project(): jnp.einsum('pqy,qk->pyk', data_block, table, precision=lax.Precision.HIGH...  73.4 us
    dot_general x2, matrix products, add_block(): jnp.einsum('tna,tnb->tab', weight_x, weight_y, preferred_element_type=jnp...  39.5 us
    psum x4, blocking collectives, over_axes(): value = lax.psum(value, axis)  38.8 us
    all_to_all x2, starting transfers between devices, one_exchange(): parts = lax.all_to_all(parts, axis, split_axis=0, concat_axis=0, tiled=True)  25 us
    dot_general x1, matrix products, local(): jnp.dot(flat_rows, jnp.sin(angle_y), precision=lax.Precision.HIGHEST)  18 us
    cos x1, other arithmetic, local(): jnp.cos(angle_y)  17.5 us
  transfers between devices with their start and end apart: 9, of which 5 were waited for; matrix products, arithmetic and copies ran while one was open for 9% of the time, Pallas kernels for 0%

commit v1 on v0

v1 whole, which is shorter than its diff:
```python
import functools
import math

import jax
import jax.numpy as jnp
import numpy as np
from jax import lax
from jax.experimental import pallas as pl
from jax.experimental.pallas import tpu as pltpu
from jax.sharding import Mesh
from jax.sharding import PartitionSpec as P

NX = 1024
NY = 1024
PLANES = 8
BETA = 18.4
OWNERS = 32
RX = 32
TILE = 128
NT = (((1,), (1,)), ((), ()))


def tap_values(step, fraction):
    z = (step.astype(jnp.float32) - fraction) * 0.25
    return jnp.exp(BETA * (jnp.sqrt(1.0 - z * z) - 1.0))


def spread_kernel(
    bucket_ref, cell_ref, fx_ref, fy_ref, mass_ref, live_ref,
    main_ref, rim_ref, total_ref,
    grid_acc, rim_acc, lx_s, ly_s, fx_s, fy_s, w_s,
):
    tiles = cell_ref.shape[0]
    zero = jnp.zeros((8, TILE), jnp.float32)

    def clear(i, _):
        for p in range(PLANES):
            grid_acc[p, pl.ds(pl.multiple_of(i * 8, 8), 8), :] = zero
        return 0

    lax.fori_loop(0, grid_acc.shape[1] // 8, clear, 0)

    def clear_rim(i, _):
        for p in range(8):
            rim_acc[i * 8 + p] = zero
        return 0

    lax.fori_loop(0, OWNERS, clear_rim, 0)

    def prepare(i, _):
        rows = pl.ds(pl.multiple_of(i * 16, 16), 16)
        cell = cell_ref[rows, :]
        ly_s[rows, :] = cell & 127
        lx_s[rows, :] = (cell >> 7) & 31
        fx_s[rows, :] = fx_ref[rows, :].astype(jnp.float32)
        fy_s[rows, :] = fy_ref[rows, :].astype(jnp.float32)
        w_s[rows, :] = jnp.where(live_ref[rows, :] == 1, mass_ref[rows, :].astype(jnp.float32), 0.0)
        return 0

    lax.fori_loop(0, tiles // 16, prepare, 0)

    sub = lax.broadcasted_iota(jnp.int32, (8, TILE), 0)

    def row(ref, t):
        return jnp.broadcast_to(ref[pl.ds(t, 1), :], (8, TILE))

    def one_tile(t):
        lx, ly = row(lx_s, t), row(ly_s, t)
        jx = (sub - lx + 3) & 7
        jy = (sub - ly + 3) & 7
        tx = tap_values(jx - 3, row(fx_s, t))
        ty = tap_values(jy - 3, row(fy_s, t)) * row(w_s, t)
        gx = (lx + jx + 5) >> 3
        gy = (ly + jy - 3) >> 3
        gy = jnp.where(gy < 0, 16, gy)
        wx = jnp.concatenate([jnp.where(gx == g, tx, 0.0) for g in range(6)]).astype(jnp.bfloat16)
        wy = jnp.concatenate([jnp.where(gy == g, ty, 0.0) for g in range(16)]).astype(jnp.bfloat16)
        wr = jnp.concatenate([jnp.where(gy == 16, ty, 0.0), zero]).astype(jnp.bfloat16)
        main = lax.dot_general(wx, wy, NT, preferred_element_type=jnp.float32)
        rim = lax.dot_general(wr, wx, NT, preferred_element_type=jnp.float32)
        return main, rim[:8]

    unroll = 8

    def add_tiles(i, _):
        results = [one_tile(i * unroll + k) for k in range(unroll)]
        for k in range(unroll):
            bucket = bucket_ref[i * unroll + k]
            owner, plane = bucket >> 3, bucket & 7
            main, rim = results[k]
            rows = pl.ds(pl.multiple_of(owner * RX, RX), 48)
            grid_acc[plane, rows, :] = grid_acc[plane, rows, :] + main
            rim_acc[bucket, :, :48] = rim_acc[bucket, :, :48] + rim
        return 0

    lax.fori_loop(0, tiles // unroll, add_tiles, 0)

    for p in range(PLANES):
        grid_acc[p, 1024:1032, :] = grid_acc[p, 1024:1032, :] + grid_acc[p, 0:8, :]
        grid_acc[p, 8:16, :] = grid_acc[p, 8:16, :] + grid_acc[p, 1032:1040, :]

    lane = lax.broadcasted_iota(jnp.int32, (8, TILE), 1)

    def write_out(i, total):
        rows = pl.ds(pl.multiple_of(i * RX + 8, 8), RX)
        for p in range(PLANES):
            block = grid_acc[p, rows, :]
            main_ref[p, i // 2, i % 2] = block
            for k in range(RX // 8):
                total = total + block[8 * k : 8 * k + 8, :]
        before, after = (i + OWNERS - 1) % OWNERS, (i + 1) % OWNERS
        for q in range(2):
            out = zero
            for k in range(4):
                p = 4 * q + k
                own = pltpu.roll(rim_acc[i * 8 + p], (32 * k - 8) % 128, 1)
                low = pltpu.roll(rim_acc[before * 8 + p], (32 * k - 40) % 128, 1)
                high = pltpu.roll(rim_acc[after * 8 + p], (32 * k + 24) % 128, 1)
                spot = lane - 32 * k
                out = jnp.where((spot >= 0) & (spot < 32), own, out)
                out = out + jnp.where((spot >= 0) & (spot < 8), low, 0.0)
                out = out + jnp.where((spot >= 24) & (spot < 32), high, 0.0)
            rim_ref[q, i // 2, i % 2] = out
            total = total + out
        return total

    total_ref[...] = lax.fori_loop(0, OWNERS, write_out, zero)


def spread(buckets, cells, fx, fy, mass, live):
    tiles = cells.shape[0]
    vmem = pl.BlockSpec(memory_space=pltpu.VMEM)
    return pl.pallas_call(
        spread_kernel,
        out_shape=(
            jax.ShapeDtypeStruct((PLANES, 16, 2, RX, TILE), jnp.float32),
            jax.ShapeDtypeStruct((2, 16, 2, 8, TILE), jnp.float32),
            jax.ShapeDtypeStruct((8, TILE), jnp.float32),
        ),
        in_specs=[pl.BlockSpec(memory_space=pltpu.SMEM)] + [vmem] * 5,
        out_specs=(vmem, vmem, vmem),
        scratch_shapes=[
            pltpu.VMEM((PLANES, NX + 16, TILE), jnp.float32),
            pltpu.VMEM((OWNERS * PLANES, 8, TILE), jnp.float32),
            pltpu.VMEM((tiles, TILE), jnp.int32),
            pltpu.VMEM((tiles, TILE), jnp.int32),
            pltpu.VMEM((tiles, TILE), jnp.float32),
            pltpu.VMEM((tiles, TILE), jnp.float32),
            pltpu.VMEM((tiles, TILE), jnp.float32),
        ],
        name="spread",
    )(buckets, cells, fx, fy, mass, live)


COORDS = ("px_0", "px_1", "px_2")


def near(v):
    return v + 1 - 2 * (v % 2)


def far(v):
    return 3 - v


ROUTES = (("x", "near"), ("x", "far"), ("y", "near"), ("y", "far"))


def reduce_kernel(
    main_ref, rim_ref, total_ref, counts_ref,
    main_out, rim_out, total_out, start_out,
    main0, rim0, main1, rim1, main2, rim2, main3, rim3, main4, rim4,
    note, notes, note_send, note_recv, send, recv,
):
    x, y, c = (lax.axis_index(a) for a in COORDS)
    me = (x * 4 + y) * 2 + c
    barrier = pltpu.get_barrier_semaphore()

    def place(index):
        return {"px_0": index // 8, "px_1": index // 2 % 4, "px_2": index % 2}

    def greet(k, _):
        pl.semaphore_signal(
            barrier, inc=1, device_id=place((me + k) % OWNERS), device_id_type=pl.DeviceIdType.MESH
        )
        return 0

    lax.fori_loop(1, OWNERS, greet, 0)
    note[0:1, :] = counts_ref[0, :, 0:TILE].astype(jnp.float32)
    note[1:2, :] = counts_ref[0, :, TILE:].astype(jnp.float32)
    note[2:3, :] = jnp.sum(total_ref[...], axis=0, keepdims=True)
    note[3:8, :] = jnp.zeros((5, TILE), jnp.float32)
    notes[me] = note[...]
    pl.semaphore_wait(barrier, OWNERS - 1)

    def remote(src, dst, slot, where):
        copy = pltpu.make_async_remote_copy(
            src_ref=src, dst_ref=dst, send_sem=send.at[slot], recv_sem=recv.at[slot],
            device_id=where, device_id_type=pl.DeviceIdType.MESH,
        )
        copy.start()
        return copy

    chunks = []
    for k in range(10):
        if k < 8:
            refs = (main_ref.at[k], *(r.at[k] for r in (main0, main1, main2, main3, main4)), main_out.at[k])
        else:
            refs = (rim_ref.at[k - 8], *(r.at[k - 8] for r in (rim0, rim1, rim2, rim3, rim4)), rim_out.at[k - 8])
        chunks.append((*refs, k % 4 if k < 8 else 2 * (k - 8)))

    def leg(first, kind):
        v = x if first == "x" else y
        if kind == "near":
            low = (v + 1) // 2 % 2
            keep, give = (low, 3 - low), (1 - low, 2 + low)
            partner, other = near(v), far(v)
        else:
            low = 2 * (v // 2)
            keep, give = (low, low + 1), (2 - low, 3 - low)
            partner, other = far(v), near(v)
        axis = "px_0" if first == "x" else "px_1"
        return keep, give, {axis: partner}, other, {axis: other}

    pending = {}
    for k, (src, b0, *_) in enumerate(chunks):
        pending[k] = [remote(src.at[:, :, 1 - c], b0, 6 * k, {"px_2": 1 - c})]

    def tell(k, _):
        peer = (me + k) % OWNERS
        pltpu.make_async_remote_copy(
            src_ref=note, dst_ref=notes.at[me], send_sem=note_send.at[peer], recv_sem=note_recv.at[me],
            device_id=place(peer), device_id_type=pl.DeviceIdType.MESH,
        ).start()
        return 0

    lax.fori_loop(1, OWNERS, tell, 0)
    sent = []

    def arrive(k):
        for copy in pending[k]:
            copy.wait_recv()
        sent.extend(pending[k])

    for k, (src, b0, b1, b2, b3, b4, out, route) in enumerate(chunks):
        arrive(k)

        def add0(i, _, src=src, b0=b0):
            for j in range(4):
                b0[i, j] = b0[i, j] + src[i, j, c]
            return 0

        lax.fori_loop(0, 4, add0, 0)
        first, kind = ROUTES[route]
        _, give, where, _, _ = leg(first, kind)
        pending[k] = []
        for n in range(2):
            block = b0.at[give[n]] if first == "x" else b0.at[:, give[n]]
            pending[k].append(remote(block, b1.at[n], 6 * k + 1 + n, where))

    for k, (src, b0, b1, b2, b3, b4, out, route) in enumerate(chunks):
        arrive(k)
        first, kind = ROUTES[route]
        keep, _, _, other, where = leg(first, kind)
        for n in range(2):
            for j in range(4):
                at = (keep[n], j) if first == "x" else (j, keep[n])
                b0[at] = b0[at] + b1[n, j]
        block = b0.at[other] if first == "x" else b0.at[:, other]
        pending[k] = [remote(block, b2, 6 * k + 3, where)]

    for k, (src, b0, b1, b2, b3, b4, out, route) in enumerate(chunks):
        arrive(k)
        first, kind = ROUTES[route]
        for j in range(4):
            at = (x, j) if first == "x" else (j, y)
            b0[at] = b0[at] + b2[j]
        second = "y" if first == "x" else "x"
        _, give, where, _, _ = leg(second, kind)
        pending[k] = []
        for n in range(2):
            block = b0.at[x, give[n]] if first == "x" else b0.at[give[n], y]
            pending[k].append(remote(block, b3.at[n], 6 * k + 4 + n, where))

    last = 6 * len(chunks)
    for k, (src, b0, b1, b2, b3, b4, out, route) in enumerate(chunks):
        arrive(k)
        first, kind = ROUTES[route]
        second = "y" if first == "x" else "x"
        keep, _, _, other, where = leg(second, kind)
        for n in range(2):
            at = (x, keep[n]) if first == "x" else (keep[n], y)
            b0[at] = b0[at] + b3[n]
        block = b0.at[x, other] if first == "x" else b0.at[other, y]
        pending[k] = [remote(block, b4, last + k, where)]

    def heard(k, _):
        peer = (me + k) % OWNERS
        copy = pltpu.make_async_remote_copy(
            src_ref=note, dst_ref=notes.at[peer], send_sem=note_send.at[peer], recv_sem=note_recv.at[peer],
            device_id=place(peer), device_id_type=pl.DeviceIdType.MESH,
        )
        copy.wait_send()
        copy.wait_recv()
        return 0

    lax.fori_loop(1, OWNERS, heard, 0)
    everyone = jnp.zeros((8, TILE), jnp.float32)
    earlier = jnp.zeros((8, TILE), jnp.float32)
    for i in range(OWNERS):
        part = notes[i]
        everyone = everyone + part
        earlier = earlier + jnp.where(i < me, part, 0.0)
    lane = lax.broadcasted_iota(jnp.int32, (8, TILE), 1)
    running = everyone
    for shift in (1, 2, 4, 8, 16, 32, 64):
        running = running + jnp.where(lane >= shift, pltpu.roll(running, shift, 1), 0.0)
    begin = running - everyone + earlier
    whole = jnp.sum(everyone[0:1, :], axis=1, keepdims=True)
    start_out[0, :, 0:TILE] = begin[0:1, :].astype(jnp.int32)
    start_out[0, :, TILE:] = (begin[1:2, :] + whole).astype(jnp.int32)
    total_out[...] = jnp.broadcast_to(everyone[2:3, :], (8, TILE))

    for k, (src, b0, b1, b2, b3, b4, out, route) in enumerate(chunks):
        arrive(k)
        out[...] = b0[x, y] + b4[...]
    for copy in sent:
        copy.wait_send()


def reduce_rows(main, rim, total, counts):
    vmem = pl.BlockSpec(memory_space=pltpu.VMEM)
    f32 = jnp.float32

    def both(*lead):
        return [pltpu.VMEM((PLANES, *lead, RX, TILE), f32), pltpu.VMEM((2, *lead, 8, TILE), f32)]

    return pl.pallas_call(
        reduce_kernel,
        out_shape=(
            jax.ShapeDtypeStruct((PLANES, RX, TILE), f32),
            jax.ShapeDtypeStruct((2, 8, TILE), f32),
            jax.ShapeDtypeStruct((8, TILE), f32),
            jax.ShapeDtypeStruct((1, 1, 2 * TILE), jnp.int32),
        ),
        in_specs=[vmem] * 4,
        out_specs=(vmem,) * 4,
        scratch_shapes=[
            *both(4, 4), *both(2, 4), *both(4), *both(2), *both(),
            pltpu.VMEM((8, TILE), f32),
            pltpu.VMEM((OWNERS, 8, TILE), f32),
            pltpu.SemaphoreType.DMA((OWNERS,)),
            pltpu.SemaphoreType.DMA((OWNERS,)),
            pltpu.SemaphoreType.DMA((70,)),
            pltpu.SemaphoreType.DMA((70,)),
        ],
        compiler_params=pltpu.CompilerParams(collective_id=0, has_side_effects=True),
        name="reduce_rows",
    )(main, rim, total, counts)


PX = ("px_0", "px_1", "px_2")
PX_PY = ("px_0", "px_1", "px_2", "py")


def passed_along(value, axis, steps):
    count = lax.axis_size(axis)
    pairs = [(source, (source + steps) % count) for source in range(count)]
    return lax.ppermute(value, axis, pairs)


def in_blocks(value, dim, devices):
    before, after = (value.shape[:dim], value.shape[dim + 1 :])
    return jnp.moveaxis(value.reshape(*before, devices, -1, *after), dim, 0)


def laid_out(parts, dim):
    lengths = list(parts.shape[1:])
    lengths[dim] *= parts.shape[0]
    return jnp.moveaxis(parts, 0, dim).reshape(lengths)


def one_exchange(value, axis, axes, splits, concats):
    sizes = [lax.axis_size(a) for a in axes]
    parts = in_blocks(value, splits[0], sizes[0])
    parts = jnp.moveaxis(in_blocks(parts, splits[1] + 1, sizes[1]), 0, 1)
    inside = parts.shape[2:]
    parts = parts.reshape(-1, *inside)
    parts = lax.all_to_all(parts, axis, split_axis=0, concat_axis=0, tiled=True)
    parts = laid_out(parts.reshape(*sizes, *inside), concats[0] + 1)
    return laid_out(parts, concats[1])


def fold_columns(extended, col_count):
    core = extended[:, :, 4 : col_count + 4]
    for direction in (1, -1):
        if direction == 1:
            rim_cells = extended[:, :, col_count + 4 :]
        else:
            rim_cells = extended[:, :, :4]
        moved = passed_along(rim_cells, "py", direction)
        if direction == 1:
            core = core.at[:, :, :4].add(moved)
        else:
            core = core.at[:, :, col_count - 4 :].add(moved)
    return core


def project(data_block, table):
    return jnp.einsum("pqy,qk->pyk", data_block, table, precision=lax.Precision.HIGHEST)


def local(cell_ids, offset_x, offset_y, mass, live, tile_owner, counts):
    px_count = lax.axis_size(PX)
    py_count = lax.axis_size("py")
    row_count = NX // px_count
    col_count = NY // py_count
    tile_cells = cell_ids[0]
    buckets = tile_owner[0] * PLANES + tile_cells[:, 0] // 4096
    main, rim, total = spread(buckets, tile_cells, offset_x[0], offset_y[0], mass[0], live[0])
    main, rim, total, bucket_start = reduce_rows(
        main.reshape(PLANES, 4, 4, 2, row_count, col_count), rim.reshape(2, 4, 4, 2, 8, 128), total, counts
    )
    rim = rim.reshape(2, 8, 4, 32).transpose(0, 2, 3, 1).reshape(PLANES, row_count, 8)
    left = jnp.concatenate([jnp.zeros_like(rim[:, :, :5]), rim[:, :, 5:]], axis=2)[:, :, 4:]
    density = fold_columns(jnp.concatenate([left, main, rim[:, :, :4]], axis=2), col_count)
    grand_total = lax.psum(jnp.sum(total[0]), "py")
    contrast = density / (grand_total / (PLANES * NX * NY)) - 1.0
    by_rows = lax.all_to_all(contrast, "py", split_axis=1, concat_axis=2, tiled=True)
    part_rows = by_rows.shape[1]
    freq_y = jnp.arange(NY, dtype=jnp.int32)
    angle_y = 2.0 * math.pi / NY * (freq_y[:, None] * freq_y[None, :] % NY).astype(jnp.float32)
    flat_rows = by_rows.reshape(-1, NY)
    real_y = jnp.dot(flat_rows, jnp.cos(angle_y), precision=lax.Precision.HIGHEST).reshape(
        by_rows.shape
    )
    imag_y = -jnp.dot(flat_rows, jnp.sin(angle_y), precision=lax.Precision.HIGHEST).reshape(
        by_rows.shape
    )
    real_cols, imag_cols = (
        one_exchange(real_y, PX_PY, (PX, "py"), (2, 2), (1, 1)),
        one_exchange(imag_y, PX_PY, (PX, "py"), (2, 2), (1, 1)),
    )
    row_order = jnp.arange(NX, dtype=jnp.int32)
    within = row_order % part_rows
    from_px = row_order // part_rows % px_count
    from_py = row_order // (part_rows * px_count)
    true_x = from_px * row_count + from_py * part_rows + within
    angle_x = 2.0 * math.pi / NX * (true_x[:, None] * row_order[None, :] % NX).astype(jnp.float32)
    cos_x = jnp.cos(angle_x)
    sin_x = jnp.sin(angle_x)
    out_real = project(real_cols, cos_x) + project(imag_cols, sin_x)
    out_imag = project(imag_cols, cos_x) - project(real_cols, sin_x)
    spectrum = jnp.stack([out_real, out_imag]) * (1.0 / math.sqrt(NX * NY))
    return (spectrum, bucket_start)


def solution(mesh):
    torus = Mesh(mesh.devices.reshape(4, 4, 2, mesh.shape["py"]), ("px_0", "px_1", "px_2", "py"))
    return jax.shard_map(
        local,
        mesh=torus,
        in_specs=(
            P(PX, "py", None),
            P(PX, "py", None),
            P(PX, "py", None),
            P(PX, "py", None),
            P(PX, "py", None),
            P(PX, "py"),
            P(PX, "py", None),
        ),
        out_specs=(P(None, None, PX_PY, None), P(PX, "py", None)),
        check_vma=False,
    )
```

time: 523 us -> 296 us (0.57); the launches traced: 513 us -> 291 us
  other arithmetic: 134 us -> 24.9 us
  waiting for transfers between devices: 96.3 us -> 3.68 us
  Pallas kernels: 0 us -> 67.7 us
  matrix products: 142 us -> 103 us
  blocking collectives: 38.8 us -> 13.1 us
  between operations: 15.4 us -> 1.95 us
    scatter-add x4 -> x0, other arithmetic: 107 us -> none  [the longest x2 106 us: add_block(): return (running.at[block_slot].add(contrib), None)]
    reduce_scatter x1 -> x0, waiting for transfers between devices: 80.8 us -> none  [local(): extended = lax.psum_scatter(blocks, PX, scatter_dimension=0, tiled=True)[0]]
    pallas_call x0 -> x2, Pallas kernels: none -> 67.7 us  [the longest x1 37.5 us: spread(): pl.pallas_call(spread_kernel, out_shape=(jax.ShapeDtypeStruct((PLANES, 16...]
    dot_general x2 -> x0, matrix products: 39.5 us -> none  [add_block(): jnp.einsum('tna,tnb->tab', weight_x, weight_y, preferred_element_type=jnp...]
    psum x4 -> x1, blocking collectives: 38.8 us -> 13.1 us  [local(): grand_total = lax.psum(jnp.sum(total[0]), 'py')]
    all_to_all x1 -> x0, starting transfers between devices: 8.97 us -> none  [from_everyone(): lax.all_to_all(jnp.broadcast_to(value[None], (devices, *value.shape)), ax...]
    all_to_all x2, starting transfers between devices: 25 us -> 32.7 us  [one_exchange(): parts = lax.all_to_all(parts, axis, split_axis=0, concat_axis=0, tiled=True)]
    all_to_all x1, waiting for transfers between devices: 7.56 us -> 0.01 us  [local(): lax.all_to_all(contrast, 'py', split_axis=1, concat_axis=2, tiled=True)]
  transfers between devices with their start and end apart: 9 -> 5, of which waited for: 5 -> 1; matrix products, arithmetic and copies ran while one was open for 9% -> 16% of each run, Pallas kernels for 0% -> 0%
where the time goes in v1:
time: 296 us; the launch traced here: 291 us
  matrix products  103 us (35%)
  Pallas kernels  67.7 us (23%)
  starting transfers between devices  42.5 us (14%)
  local copies, waits for them, and re-layouts  34.9 us (12%)
  other arithmetic  24.9 us (8%)
  blocking collectives  13.1 us (4%)
  waiting for transfers between devices  3.68 us (1%)
    dot_general x4, matrix products, project(): jnp.einsum('pqy,qk->pyk', data_block, table, precision=lax.Precision.HIGH...  73.4 us
    pallas_call x1, Pallas kernels, spread(): pl.pallas_call(spread_kernel, out_shape=(jax.ShapeDtypeStruct((PLANES, 16...  37.5 us
    all_to_all x2, starting transfers between devices, one_exchange(): parts = lax.all_to_all(parts, axis, split_axis=0, concat_axis=0, tiled=True)  32.7 us
    pallas_call x1, Pallas kernels, reduce_rows(): pl.pallas_call(reduce_kernel, out_shape=(jax.ShapeDtypeStruct((PLANES, RX...  30.2 us
    dot_general x1, matrix products, local(): jnp.dot(flat_rows, jnp.sin(angle_y), precision=lax.Precision.HIGHEST)  18 us
    cos x1, other arithmetic, local(): jnp.cos(angle_y)  17.5 us
    psum x1, blocking collectives, local(): grand_total = lax.psum(jnp.sum(total[0]), 'py')  13.1 us
    unnamed x8, local copies, waits for them, and re-layouts  12.5 us
  transfers between devices with their start and end apart: 5, of which 1 were waited for; matrix products, arithmetic and copies ran while one was open for 16% of the time, Pallas kernels for 0%

profile of v1, /device:TPU:1, one launch (start us, length us, event | category | flops | bytes accessed | tf_op | source)
XLA Modules:
  0.0 291.2 jit_solution(6529412390077513530)
XLA Ops:
  3.1 37.5 %spread.1 = (f32[8,16,2,32,128]{4,3,2,1,0:T(8,128)}, f32[2,16,2,8,128]{4,3,2,1,0:T(8,128)}, f32[8,128]{1,0:T(8,128)}) custom-call(s32[640]{0:T(1024)} %fusion.72.bucket_ref, s32[640,128]{1,0:T(8,128)} %bitcast.106, bf16[640,128]{1,0:T(8,128)(2,1)} %bitcast.113, bf16[640,128]{1,0:T(8,128)(2,1)} %bitcast.114, bf16[640,128]{1,0:T(8,128)(2,1)} %bitcast.115, ...), custom_call_target="tpu_custom_call" | custom-call | tf_op jit(solution)/shard_map/spread/pallas_call | solution.py:133
  40.5 30.2 %reduce_rows.1 = (f32[8,32,128]{2,1,0:T(8,128)}, f32[2,8,128]{2,1,0:T(8,128)}, f32[8,128]{1,0:T(8,128)}, s32[1,1,256]{2,1,0:T(1,128)}) custom-call(f32[8,4,4,2,32,128]{5,4,3,2,1,0:T(8,128)} %bitcast.102, f32[2,4,4,2,8,128]{5,4,3,2,1,0:T(8,128)} %bitcast.112, f32[8,128]{1,0:T(8,128)} %get-tuple-element.35.total_ref, s32[1,1,256]{2,1,0:T(1,128)} %counts_ref.1), custom_call_target="tpu_custom_call" | custom-call | tf_op jit(solution)/shard_map/reduce_rows/pallas_call | solution.py:338
  73.6 4.0 %collective-permute-start.1 = (f32[8,32,4]{2,1,0:T(8,128)S(1)}, f32[8,32,4]{2,1,0:T(8,128)S(1)}, u32[]{:S(2)}, u32[]{:S(2)}) collective-permute-start(f32[8,32,4]{2,1,0:T(8,128)S(1)} %pad_slice_fusion), channel_id=1, source_target_pairs={{0,7},{1,0},{2,1},{3,2},{4,3},{5,4},{6,5},{7,6},{8,15},{9,8},{10,9... | collective-permute-start | bytes 12296 | tf_op jit(solution)/shard_map/ppermute | solution.py:369
  78.9 13.1 %psum.7 = f32[]{:T(128)} all-reduce(f32[]{:T(128)} %slice_reduce_fusion.1), channel_id=1, replica_groups=mesh['px_0'=4,'px_1'=4,'px_2'=2,'py'=8] {'py'}, use_global_device_ids=true, to_apply=%region_1.2 | all-reduce | flops 1 | bytes 8 | tf_op jit(solution)/shard_map/psum | solution.py:427
  100.1 4.0 %all-to-all-start = ((f32[8,32,128]{2,0,1:T(8,128)}), f32[8,32,128]{2,0,1:T(8,128)S(1)}, u32[]{:S(2)}, u32[]{:S(2)}) async-start(f32[8,32,128]{2,0,1:T(8,128)} %copy.34), calls=%async_computation | async-start | bytes 262144 | tf_op jit(solution)/shard_map/all_to_all | solution.py:429
  104.1 17.5 %fusion.3 = f32[1024,1024]{1,0:T(8,128)} fusion(s32[1024]{0:T(1024)S(1)} %mul.144), kind=kLoop, calls=%fused_computation.12 | loop fusion | flops 14680064 | bytes 4198400 | tf_op jit(solution)/shard_map/cos | solution.py:434
  121.6 18.0 %fusion.54 = f32[8,4,1024]{2,0,1:T(8,128)S(1)} fusion(f32[8,8,4,128]{3,0,2,1:T(8,128)S(1)} %bitcast.107), kind=kOutput, calls=%fused_computation.50 | convolution fusion | flops 417366016 | bytes 262144 | tf_op jit(solution)/shard_map/dot_general | solution.py:437
  140.0 2.3 copy.53
  142.3 3.1 %reshape.218 = f32[256,1,128]{2,1,0:T(1,128)} reshape(f32[256,4,4,8]{3,2,1,0:T(4,128)S(1)} %bitcast.96) | data formatting | bytes 262144
  145.4 18.5 %all-to-all-start.2 = ((f32[256,1,128]{2,1,0:T(1,128)}), f32[256,1,128]{2,1,0:T(1,128)S(1)}, u32[]{:S(2)}, u32[]{:S(2)}) async-start(f32[256,1,128]{2,1,0:T(1,128)} %reshape.218), calls=%async_computation.2 | async-start | bytes 262144 | tf_op jit(solution)/shard_map/all_to_all | solution.py:389
  163.9 11.3 %convolution_bitcast_fusion = f32[32,8,4,32]{3,1,0,2:T(8,128)S(1)} fusion(f32[32,32,1024,1]{2,1,0,3:T(8,128)} %bitcast.95, f32[8,8,4,128]{3,0,2,1:T(8,128)S(1)} %bitcast.108), kind=kOutput, calls=%fused_computation.45 | convolution fusion | flops 402653184 | bytes 4456448 | tf_op jit(solution)/shard_map/dot_general | solution.py:434
  175.4 2.3 copy.50
  177.8 3.1 %reshape.216 = f32[256,1,128]{2,1,0:T(1,128)} reshape(f32[256,4,4,8]{3,2,1,0:T(4,128)S(1)} %bitcast.97) | data formatting | bytes 262144
  180.9 14.2 %all-to-all-start.1 = ((f32[256,1,128]{2,1,0:T(1,128)}), f32[256,1,128]{2,1,0:T(1,128)S(1)}, u32[]{:S(2)}, u32[]{:S(2)}) async-start(f32[256,1,128]{2,1,0:T(1,128)} %reshape.216), calls=%async_computation.1 | async-start | bytes 262144 | tf_op jit(solution)/shard_map/all_to_all | solution.py:389
  196.5 2.5 reshape.219
  199.0 2.2 copy.55
  201.2 2.6 copy.47
  203.9 3.7 %all-to-all-done.1 = f32[256,1,128]{2,1,0:T(1,128)S(1)} async-done(((f32[256,1,128]{2,1,0:T(1,128)}), f32[256,1,128]{2,1,0:T(1,128)S(1)}, u32[]{:S(2)}, u32[]{:S(2)}) %all-to-all-start.1) | async-done | bytes 131104 | tf_op jit(solution)/shard_map/all_to_all | solution.py:389
  208.5 2.5 reshape.217
  213.2 2.6 copy.41
  215.9 18.4 %fusion.16 = f32[8,4,1024]{2,0,1:T(8,128)S(1)} fusion(s32[1024]{0:T(1024)S(1)} %fusion.76, f32[8,8,128,4]{2,0,1,3:T(8,128)S(1)} %copy.47), kind=kOutput, calls=%fused_computation.24 | convolution fusion | flops 417333248 | bytes 266240 | tf_op jit(solution)/shard_map/pqy,qk->pyk/dot_general | solution.py:410
  234.3 18.4 %fusion.14 = f32[8,4,1024]{2,0,1:T(8,128)S(1)} fusion(s32[1024]{0:T(1024)S(1)} %fusion.76, f32[8,8,128,4]{2,0,1,3:T(8,128)S(1)} %copy.41), kind=kOutput, calls=%fused_computation.22 | convolution fusion | flops 417333248 | bytes 266240 | tf_op jit(solution)/shard_map/pqy,qk->pyk/dot_general | solution.py:410
  252.7 18.3 %fusion.45 = f32[1,8,4,1024]{3,1,2,0:T(8,128)S(1)} fusion(f32[8,4,1024]{2,0,1:T(8,128)S(1)} %fusion.16, s32[1024]{0:T(1024)S(1)} %fusion.76, f32[8,8,128,4]{2,0,1,3:T(8,128)S(1)} %copy.41), kind=kOutput, calls=%fused_computation.47 | convolution fusion | flops 417366016 | bytes 397312 | tf_op jit(solution)/shard_map/pqy,qk->pyk/dot_general | solution.py:410
  271.1 18.2 %fusion.51 = f32[1,8,4,1024]{3,1,2,0:T(8,128)S(1)} fusion(f32[8,4,1024]{2,0,1:T(8,128)S(1)} %fusion.14, s32[1024]{0:T(1024)S(1)} %fusion.76, f32[8,8,128,4]{2,0,1,3:T(8,128)S(1)} %copy.47), kind=kOutput, calls=%fused_computation.49 | convolution fusion | flops 417366016 | bytes 397312 | tf_op jit(solution)/shard_map/pqy,qk->pyk/dot_general | solution.py:410
  (34 shorter events, 20.7 us)
Async XLA Ops:
  71.7 21.0 %collective-permute-start = (f32[8,32,4]{2,1,0:T(8,128)S(1)}, f32[8,32,4]{2,1,0:T(8,128)S(1)}, u32[]{:S(2)}, u32[]{:S(2)}) collective-permute-start(f32[8,32,4]{2,1,0:T(8,128)S(1)} %bitcast.109), channel_id=1, source_target_pairs={{0,1},{1,2},{2,3},{3,4},{4,5},{5,6},{6,7},{7,0},{8,9},{9,10},{10,1... | collective-permute-start | bytes 12296 | tf_op jit(solution)/shard_map/ppermute | solution.py:369
  73.6 21.7 %collective-permute-start.1 = (f32[8,32,4]{2,1,0:T(8,128)S(1)}, f32[8,32,4]{2,1,0:T(8,128)S(1)}, u32[]{:S(2)}, u32[]{:S(2)}) collective-permute-start(f32[8,32,4]{2,1,0:T(8,128)S(1)} %pad_slice_fusion), channel_id=1, source_target_pairs={{0,7},{1,0},{2,1},{3,2},{4,3},{5,4},{6,5},{7,6},{8,15},{9,8},{10,9... | collective-permute-start | bytes 12296 | tf_op jit(solution)/shard_map/ppermute | solution.py:369
  100.1 21.5 %all-to-all-start = ((f32[8,32,128]{2,0,1:T(8,128)}), f32[8,32,128]{2,0,1:T(8,128)S(1)}, u32[]{:S(2)}, u32[]{:S(2)}) async-start(f32[8,32,128]{2,0,1:T(8,128)} %copy.34), calls=%async_computation | async-start | bytes 262144 | tf_op jit(solution)/shard_map/all_to_all | solution.py:429
  145.4 35.5 %all-to-all-start.2 = ((f32[256,1,128]{2,1,0:T(1,128)}), f32[256,1,128]{2,1,0:T(1,128)S(1)}, u32[]{:S(2)}, u32[]{:S(2)}) async-start(f32[256,1,128]{2,1,0:T(1,128)} %reshape.218), calls=%async_computation.2 | async-start | bytes 262144 | tf_op jit(solution)/shard_map/all_to_all | solution.py:389
  180.9 26.7 %all-to-all-start.1 = ((f32[256,1,128]{2,1,0:T(1,128)}), f32[256,1,128]{2,1,0:T(1,128)S(1)}, u32[]{:S(2)}, u32[]{:S(2)}) async-start(f32[256,1,128]{2,1,0:T(1,128)} %reshape.216), calls=%async_computation.1 | async-start | bytes 262144 | tf_op jit(solution)/shard_map/all_to_all | solution.py:389
  271.1 19.1 %copy-start = (s32[1,1,256]{2,1,0:T(1,128)S(1)}, s32[1,1,256]{2,1,0:T(1,128)}, u32[]{:S(2)}) copy-start(s32[1,1,256]{2,1,0:T(1,128)} %get-tuple-element.51) | copy-start | bytes 3076

commit v2 on v1

--- a/solution.py
+++ b/solution.py
@@ -168,7 +168,7 @@
 
 def reduce_kernel(
     main_ref, rim_ref, total_ref, counts_ref,
-    main_out, rim_out, total_out, start_out,
+    pack_out, start_out,
     main0, rim0, main1, rim1, main2, rim2, main3, rim3, main4, rim4,
     note, notes, note_send, note_recv, send, recv,
 ):
@@ -204,9 +204,9 @@
     chunks = []
     for k in range(10):
         if k < 8:
-            refs = (main_ref.at[k], *(r.at[k] for r in (main0, main1, main2, main3, main4)), main_out.at[k])
+            refs = (main_ref.at[k], *(r.at[k] for r in (main0, main1, main2, main3, main4)), pack_out.at[k, 0:RX])
         else:
-            refs = (rim_ref.at[k - 8], *(r.at[k - 8] for r in (rim0, rim1, rim2, rim3, rim4)), rim_out.at[k - 8])
+            refs = (rim_ref.at[k - 8], *(r.at[k - 8] for r in (rim0, rim1, rim2, rim3, rim4)), None)
         chunks.append((*refs, k % 4 if k < 8 else 2 * (k - 8)))
 
     def leg(first, kind):
@@ -319,11 +319,17 @@
     whole = jnp.sum(everyone[0:1, :], axis=1, keepdims=True)
     start_out[0, :, 0:TILE] = begin[0:1, :].astype(jnp.int32)
     start_out[0, :, TILE:] = (begin[1:2, :] + whole).astype(jnp.int32)
-    total_out[...] = jnp.broadcast_to(everyone[2:3, :], (8, TILE))
+    for p in range(PLANES):
+        pack_out[p, 40:48, :] = jnp.broadcast_to(everyone[2:3, :], (8, TILE))
 
     for k, (src, b0, b1, b2, b3, b4, out, route) in enumerate(chunks):
         arrive(k)
-        out[...] = b0[x, y] + b4[...]
+        block = b0[x, y] + b4[...]
+        if k < 8:
+            pack_out[k, 0:RX, :] = block
+        else:
+            for p in range(4):
+                pack_out[4 * (k - 8) + p, RX : RX + 8, :] = block
     for copy in sent:
         copy.wait_send()
 
@@ -338,13 +344,11 @@
     return pl.pallas_call(
         reduce_kernel,
         out_shape=(
-            jax.ShapeDtypeStruct((PLANES, RX, TILE), f32),
-            jax.ShapeDtypeStruct((2, 8, TILE), f32),
-            jax.ShapeDtypeStruct((8, TILE), f32),
+            jax.ShapeDtypeStruct((PLANES, RX + 16, TILE), f32),
             jax.ShapeDtypeStruct((1, 1, 2 * TILE), jnp.int32),
         ),
         in_specs=[vmem] * 4,
-        out_specs=(vmem,) * 4,
+        out_specs=(vmem, vmem),
         scratch_shapes=[
             *both(4, 4), *both(2, 4), *both(4), *both(2), *both(),
             pltpu.VMEM((8, TILE), f32),
@@ -359,100 +363,227 @@
     )(main, rim, total, counts)
 
 
+DEVICES = 256
+
+
+def split_bf16(value):
+    high = value.astype(jnp.bfloat16)
+    return high, (value - high.astype(jnp.float32)).astype(jnp.bfloat16)
+
+
+def np_split(value):
+    high = np.asarray(value, np.float32).astype(jnp.bfloat16)
+    low = (np.asarray(value, np.float64) - high.astype(np.float64)).astype(jnp.bfloat16)
+    return high, low
+
+
+def tables():
+    k = np.arange(TILE)
+    turn_y = 2 * np.pi / NY * (np.arange(8)[:, None] * k[None, :])
+    twist_y = np.stack([np.cos(turn_y), -np.sin(turn_y)]).astype(np.float32)
+    theta = 2 * np.pi / TILE * (k[:, None] * k[None, :] % TILE)
+    wave_y = np.zeros((TILE, 2, 2, TILE))
+    wave_y[:, 0, 0], wave_y[:, 0, 1] = np.cos(theta), np.sin(theta)
+    wave_y[:, 1, 0], wave_y[:, 1, 1] = -np.sin(theta), np.cos(theta)
+    y_high, y_low = np_split(wave_y.reshape(2 * TILE, 2 * TILE))
+    phase = 2 * np.pi / OWNERS * (np.arange(OWNERS)[:, None] * k[None, :] % OWNERS)
+    block = np.zeros((OWNERS, 2, 2, TILE))
+    block[:, 0, 0], block[:, 1, 0] = np.cos(phase), np.sin(phase)
+    block[:, 0, 1], block[:, 1, 1] = -np.sin(phase), np.cos(phase)
+    wave_x = np.kron(np.eye(2), block.reshape(2 * OWNERS, 2 * TILE))
+    x_high, x_low = np_split(wave_x)
+    turn_x = 2 * np.pi / NX * (np.arange(RX)[:, None] * k[None, :])
+    scale = 1.0 / math.sqrt(NX * NY)
+    twist_x = (scale * np.stack([np.cos(turn_x), -np.sin(turn_x)])).astype(np.float32)
+    return twist_y, y_high, y_low, np.concatenate([x_high, x_high]), x_low, twist_x
+
+
+HALF = math.sqrt(0.5)
+
+
+def real_eighths(d):
+    s = [d[k] + d[k + 4] for k in range(4)]
+    e = [d[k] - d[k + 4] for k in range(4)]
+    near_sum, far_sum = s[0] + s[2], s[1] + s[3]
+    a0, a4 = near_sum + far_sum, near_sum - far_sum
+    re2, im2 = s[0] - s[2], s[3] - s[1]
+    tilt, lean = (e[1] - e[3]) * HALF, (e[1] + e[3]) * HALF
+    re1, im1 = e[0] + tilt, -e[2] - lean
+    re3, im3 = e[0] - tilt, e[2] - lean
+    zero = jnp.zeros_like(a0)
+    return [(a0, zero), (re1, im1), (re2, im2), (re3, im3), (a4, zero), (re3, -im3), (re2, -im2), (re1, -im1)]
+
+
+def fourths(t):
+    def add(p, q):
+        return p[0] + q[0], p[1] + q[1]
+
+    def less(p, q):
+        return p[0] - q[0], p[1] - q[1]
+
+    e0, e1 = add(t[0], t[2]), less(t[0], t[2])
+    f0, g = add(t[1], t[3]), less(t[1], t[3])
+    f1 = (g[1], -g[0])
+    return [add(e0, f0), add(e1, f1), less(e0, f0), less(e1, f1)]
+
+
+def eighths(z):
+    s = [(z[k][0] + z[k + 4][0], z[k][1] + z[k + 4][1]) for k in range(4)]
+    d = [(z[k][0] - z[k + 4][0], z[k][1] - z[k + 4][1]) for k in range(4)]
+    turned = [
+        d[0],
+        ((d[1][0] + d[1][1]) * HALF, (d[1][1] - d[1][0]) * HALF),
+        (d[2][1], -d[2][0]),
+        ((d[3][1] - d[3][0]) * HALF, -(d[3][0] + d[3][1]) * HALF),
+    ]
+    even, odd = fourths(s), fourths(turned)
+    return [even[0], odd[0], even[1], odd[1], even[2], odd[2], even[3], odd[3]]
+
+
+def fourier_kernel(
+    pack_ref, twist_y, y_high, y_low, x_both, x_low, twist_x,
+    out_ref,
+    got, waves, columns, send, recv, wave_send, wave_recv,
+):
+    x, y, c = (lax.axis_index(a) for a in COORDS)
+    j = lax.axis_index("py")
+    i = (x * 4 + y) * 2 + c
+    me = i * 8 + j
+    barrier = pltpu.get_barrier_semaphore()
+
+    def place(index):
+        row = index // 8
+        return {"px_0": row // 8, "px_1": row // 2 % 4, "px_2": row % 2, "py": index % 8}
+
+    def greet(k, _):
+        pl.semaphore_signal(
+            barrier, inc=1, device_id=place((me + k) % DEVICES), device_id_type=pl.DeviceIdType.MESH
+        )
+        return 0
+
+    lax.fori_loop(1, DEVICES, greet, 0)
+    got[j] = pack_ref[j]
+    pl.semaphore_wait(barrier, DEVICES - 1)
+
+    moves = []
+    for k in range(1, 8):
+        peer = (j + k) % 8
+        copy = pltpu.make_async_remote_copy(
+            src_ref=pack_ref.at[peer], dst_ref=got.at[j], send_sem=send.at[k], recv_sem=recv.at[k],
+            device_id={"py": peer}, device_id_type=pl.DeviceIdType.MESH,
+        )
+        copy.start()
+        moves.append(copy)
+    for copy in moves:
+        copy.wait()
+
+    lane = lax.broadcasted_iota(jnp.int32, (RX, TILE), 1)
+    rims = jnp.concatenate([got[s, 32:40, :] for s in range(8)])
+    rims = pltpu.roll(rims, (TILE - 32 * (j % 4)) % TILE, 1)
+    rims = jnp.concatenate([rims, jnp.zeros((64, TILE), jnp.float32)])
+    rims = jnp.transpose(rims)[:RX]
+    amount = got[0, 40:41, :]
+    for s in range(1, 8):
+        amount = amount + got[s, 40:41, :]
+    inverse = float(PLANES * NX * NY) / jnp.sum(amount, axis=1, keepdims=True)
+    blocks = []
+    for s in range(8):
+        right = pltpu.roll(rims, (-8 * ((s + 7) % 8)) % TILE, 1)
+        left = pltpu.roll(rims, (120 - 8 * ((s + 1) % 8)) % TILE, 1)
+        value = got[s, 0:32, :] + jnp.where(lane < 4, right, 0.0) + jnp.where(lane >= 125, left, 0.0)
+        blocks.append(value * inverse - 1.0)
+    turned = []
+    for k, (re, im) in enumerate(real_eighths(blocks)):
+        tr, ti = twist_y[0, k : k + 1, :], twist_y[1, k : k + 1, :]
+        turned.append(jnp.concatenate([re * tr - im * ti, re * ti + im * tr], axis=1))
+    high, low = split_bf16(jnp.concatenate(turned))
+
+    def times(a, b):
+        return lax.dot_general(a, b, NT, preferred_element_type=jnp.float32)
+
+    wave = times(y_high[...], low) + times(y_low[...], high) + times(y_high[...], high)
+    for h in range(2):
+        for k in range(TILE):
+            waves[k, h] = wave[2 * k : 2 * k + 2, TILE * h : TILE * h + TILE]
+
+    columns[j * 32 + i] = waves[me // 2, me % 2]
+
+    def hand_out(k, _):
+        peer = (me + k) % DEVICES
+        pltpu.make_async_remote_copy(
+            src_ref=waves.at[peer // 2, peer % 2], dst_ref=columns.at[j * 32 + i],
+            send_sem=wave_send, recv_sem=wave_recv,
+            device_id=place(peer), device_id_type=pl.DeviceIdType.MESH,
+        ).start()
+        return 0
+
+    lax.fori_loop(1, DEVICES, hand_out, 0)
+    others = columns.at[pl.ds(0, DEVICES - 1)]
+    pltpu.make_async_copy(others, others, wave_recv).wait()
+
+    for g in range(4):
+        pair = columns[64 * g : 64 * g + 64].reshape(TILE, TILE)
+        high, low = split_bf16(jnp.transpose(pair))
+        both = jnp.concatenate([high, low], axis=1)
+        sums = jnp.dot(both, x_both[...], preferred_element_type=jnp.float32)
+        sums = sums + jnp.dot(high, x_low[...], preferred_element_type=jnp.float32)
+        parts = [[], []]
+        for p in range(2):
+            for w in range(4):
+                re_sum = im_sum = None
+                for q in range(4):
+                    rows = slice(32 * w + 8 * q, 32 * w + 8 * q + 8)
+                    re = sums[rows, 256 * p : 256 * p + 128]
+                    im = sums[rows, 256 * p + 128 : 256 * p + 256]
+                    tr, ti = twist_x[0, 8 * q : 8 * q + 8, :], twist_x[1, 8 * q : 8 * q + 8, :]
+                    re_part, im_part = re * tr - im * ti, re * ti + im * tr
+                    re_sum = re_part if q == 0 else re_sum + re_part
+                    im_sum = im_part if q == 0 else im_sum + im_part
+                parts[0].append(re_sum)
+                parts[1].append(im_sum)
+        re, im = (jnp.transpose(jnp.stack(part), (1, 0, 2)) for part in parts)
+        for a, value in enumerate(eighths([(re[k], im[k]) for k in range(8)])):
+            for n in range(2):
+                for p in range(2):
+                    out_ref[n, 2 * g + p, :, TILE * a : TILE * a + TILE] = value[n][4 * p : 4 * p + 4]
+
+    pltpu.make_async_copy(others, others, wave_send).wait()
+
+
+def fourier(pack):
+    vmem = pl.BlockSpec(memory_space=pltpu.VMEM)
+    f32 = jnp.float32
+    return pl.pallas_call(
+        fourier_kernel,
+        out_shape=jax.ShapeDtypeStruct((2, PLANES, 4, NX), f32),
+        in_specs=[vmem] * 7,
+        out_specs=vmem,
+        scratch_shapes=[
+            pltpu.VMEM((8, 48, TILE), f32),
+            pltpu.VMEM((TILE, 2, 2, TILE), f32),
+            pltpu.VMEM((DEVICES, 2, TILE), f32),
+            pltpu.SemaphoreType.DMA((8,)),
+            pltpu.SemaphoreType.DMA((8,)),
+            pltpu.SemaphoreType.DMA,
+            pltpu.SemaphoreType.DMA,
+        ],
+        compiler_params=pltpu.CompilerParams(collective_id=1, has_side_effects=True),
+        name="fourier",
+    )(pack, *tables())
+
+
 PX = ("px_0", "px_1", "px_2")
 PX_PY = ("px_0", "px_1", "px_2", "py")
 
 
-def passed_along(value, axis, steps):
-    count = lax.axis_size(axis)
-    pairs = [(source, (source + steps) % count) for source in range(count)]
-    return lax.ppermute(value, axis, pairs)
-
-
-def in_blocks(value, dim, devices):
-    before, after = (value.shape[:dim], value.shape[dim + 1 :])
-    return jnp.moveaxis(value.reshape(*before, devices, -1, *after), dim, 0)
-
-
-def laid_out(parts, dim):
-    lengths = list(parts.shape[1:])
-    lengths[dim] *= parts.shape[0]
-    return jnp.moveaxis(parts, 0, dim).reshape(lengths)
-
-
-def one_exchange(value, axis, axes, splits, concats):
-    sizes = [lax.axis_size(a) for a in axes]
-    parts = in_blocks(value, splits[0], sizes[0])
-    parts = jnp.moveaxis(in_blocks(parts, splits[1] + 1, sizes[1]), 0, 1)
-    inside = parts.shape[2:]
-    parts = parts.reshape(-1, *inside)
-    parts = lax.all_to_all(parts, axis, split_axis=0, concat_axis=0, tiled=True)
-    parts = laid_out(parts.reshape(*sizes, *inside), concats[0] + 1)
-    return laid_out(parts, concats[1])
-
-
-def fold_columns(extended, col_count):
-    core = extended[:, :, 4 : col_count + 4]
-    for direction in (1, -1):
-        if direction == 1:
-            rim_cells = extended[:, :, col_count + 4 :]
-        else:
-            rim_cells = extended[:, :, :4]
-        moved = passed_along(rim_cells, "py", direction)
-        if direction == 1:
-            core = core.at[:, :, :4].add(moved)
-        else:
-            core = core.at[:, :, col_count - 4 :].add(moved)
-    return core
-
-
-def project(data_block, table):
-    return jnp.einsum("pqy,qk->pyk", data_block, table, precision=lax.Precision.HIGHEST)
-
-
 def local(cell_ids, offset_x, offset_y, mass, live, tile_owner, counts):
-    px_count = lax.axis_size(PX)
-    py_count = lax.axis_size("py")
-    row_count = NX // px_count
-    col_count = NY // py_count
-    tile_cells = cell_ids[0]
-    buckets = tile_owner[0] * PLANES + tile_cells[:, 0] // 4096
-    main, rim, total = spread(buckets, tile_cells, offset_x[0], offset_y[0], mass[0], live[0])
-    main, rim, total, bucket_start = reduce_rows(
-        main.reshape(PLANES, 4, 4, 2, row_count, col_count), rim.reshape(2, 4, 4, 2, 8, 128), total, counts
+    cells = cell_ids[0]
+    buckets = tile_owner[0] * PLANES + cells[:, 0] // 4096
+    main, rim, total = spread(buckets, cells, offset_x[0], offset_y[0], mass[0], live[0])
+    pack, bucket_start = reduce_rows(
+        main.reshape(PLANES, 4, 4, 2, RX, TILE), rim.reshape(2, 4, 4, 2, 8, TILE), total, counts
     )
-    rim = rim.reshape(2, 8, 4, 32).transpose(0, 2, 3, 1).reshape(PLANES, row_count, 8)
-    left = jnp.concatenate([jnp.zeros_like(rim[:, :, :5]), rim[:, :, 5:]], axis=2)[:, :, 4:]
-    density = fold_columns(jnp.concatenate([left, main, rim[:, :, :4]], axis=2), col_count)
-    grand_total = lax.psum(jnp.sum(total[0]), "py")
-    contrast = density / (grand_total / (PLANES * NX * NY)) - 1.0
-    by_rows = lax.all_to_all(contrast, "py", split_axis=1, concat_axis=2, tiled=True)
-    part_rows = by_rows.shape[1]
-    freq_y = jnp.arange(NY, dtype=jnp.int32)
-    angle_y = 2.0 * math.pi / NY * (freq_y[:, None] * freq_y[None, :] % NY).astype(jnp.float32)
-    flat_rows = by_rows.reshape(-1, NY)
-    real_y = jnp.dot(flat_rows, jnp.cos(angle_y), precision=lax.Precision.HIGHEST).reshape(
-        by_rows.shape
-    )
-    imag_y = -jnp.dot(flat_rows, jnp.sin(angle_y), precision=lax.Precision.HIGHEST).reshape(
-        by_rows.shape
-    )
-    real_cols, imag_cols = (
-        one_exchange(real_y, PX_PY, (PX, "py"), (2, 2), (1, 1)),
-        one_exchange(imag_y, PX_PY, (PX, "py"), (2, 2), (1, 1)),
-    )
-    row_order = jnp.arange(NX, dtype=jnp.int32)
-    within = row_order % part_rows
-    from_px = row_order // part_rows % px_count
-    from_py = row_order // (part_rows * px_count)
-    true_x = from_px * row_count + from_py * part_rows + within
-    angle_x = 2.0 * math.pi / NX * (true_x[:, None] * row_order[None, :] % NX).astype(jnp.float32)
-    cos_x = jnp.cos(angle_x)
-    sin_x = jnp.sin(angle_x)
-    out_real = project(real_cols, cos_x) + project(imag_cols, sin_x)
-    out_imag = project(imag_cols, cos_x) - project(real_cols, sin_x)
-    spectrum = jnp.stack([out_real, out_imag]) * (1.0 / math.sqrt(NX * NY))
-    return (spectrum, bucket_start)
+    return fourier(pack), bucket_start
 
 
 def solution(mesh):

time: 296 us -> 118 us (0.40); the launches traced: 291 us -> 117 us
  matrix products: 103 us -> 0 us
  Pallas kernels: 67.7 us -> 111 us
  starting transfers between devices: 42.5 us -> 0 us
  local copies, waits for them, and re-layouts: 34.9 us -> 4.06 us
  other arithmetic: 24.9 us -> 1.31 us
  blocking collectives: 13.1 us -> 0 us
  waiting for transfers between devices: 3.68 us -> 0 us
    dot_general x6 -> x0, matrix products: 103 us -> none  [the longest x4 73.4 us: project(): jnp.einsum('pqy,qk->pyk', data_block, table, precision=lax.Precision.HIGH...]
    pallas_call x0 -> x1, Pallas kernels: none -> 43.6 us  [fourier(): pl.pallas_call(fourier_kernel, out_shape=jax.ShapeDtypeStruct((2, PLANES,...]
    all_to_all x3 -> x0, starting transfers between devices: 36.7 us -> none  [the longest x2 32.7 us: one_exchange(): parts = lax.all_to_all(parts, axis, split_axis=0, concat_axis=0, tiled=True)]
    cos x1 -> x0, other arithmetic: 17.5 us -> none  [local(): jnp.cos(angle_y)]
    psum x1 -> x0, blocking collectives: 13.1 us -> none  [local(): grand_total = lax.psum(jnp.sum(total[0]), 'py')]
    transpose x6 -> x0, local copies, waits for them, and re-layouts: 10.1 us -> none  [the longest x4 9.75 us: laid_out(): return jnp.moveaxis(parts, 0, dim).reshape(lengths)]
    unnamed x8 -> x2, local copies, waits for them, and re-layouts: 12.5 us -> 2.92 us
    reshape x5 -> x0, local copies, waits for them, and re-layouts: 5.81 us -> none  [the longest x2 4.63 us: one_exchange(): parts = parts.reshape(-1, *inside)]
  transfers between devices with their start and end apart: 5 -> 0, of which waited for: 1 -> 0; matrix products, arithmetic and copies ran while one was open for 16% -> 0% of each run, Pallas kernels for 0% -> 0%
where the time goes in v2:
time: 118 us; the launch traced here: 117 us
  Pallas kernels  111 us (94%)
  local copies, waits for them, and re-layouts  4.06 us (3%)
  other arithmetic  1.31 us (1%)
    pallas_call x1, Pallas kernels, fourier(): pl.pallas_call(fourier_kernel, out_shape=jax.ShapeDtypeStruct((2, PLANES,...  43.6 us
    pallas_call x1, Pallas kernels, spread(): pl.pallas_call(spread_kernel, out_shape=(jax.ShapeDtypeStruct((PLANES, 16...  37.5 us
    pallas_call x1, Pallas kernels, reduce_rows(): pl.pallas_call(reduce_kernel, out_shape=(jax.ShapeDtypeStruct((PLANES, RX...  30.2 us
    unnamed x2, local copies, waits for them, and re-layouts  2.92 us

profile of v2, /device:TPU:1, one launch (start us, length us, event | category | flops | bytes accessed | tf_op | source)
XLA Modules:
  0.0 117.3 jit_solution(11377582923023938602)
XLA Ops:
  0.6 1.1 slice_reduce_fusion
  1.8 0.7 multiply_reduce_fusion
  2.5 0.6 fusion.1.bucket_ref
  3.1 37.5 %spread.1 = (f32[8,16,2,32,128]{4,3,2,1,0:T(8,128)}, f32[2,16,2,8,128]{4,3,2,1,0:T(8,128)}, f32[8,128]{1,0:T(8,128)}) custom-call(s32[640]{0:T(1024)} %fusion.1.bucket_ref, s32[640,128]{1,0:T(8,128)} %bitcast.9, bf16[640,128]{1,0:T(8,128)(2,1)} %bitcast.12, bf16[640,128]{1,0:T(8,128)(2,1)} %bitcast.13, bf16[640,128]{1,0:T(8,128)(2,1)} %bitcast.14, ...), custom_call_target="tpu_custom_call" | custom-call | tf_op jit(solution)/shard_map/spread/pallas_call | solution.py:133
  40.5 30.2 %reduce_rows.1 = (f32[8,48,128]{2,1,0:T(8,128)}, s32[1,1,256]{2,1,0:T(1,128)}) custom-call(f32[8,4,4,2,32,128]{5,4,3,2,1,0:T(8,128)} %bitcast.7, f32[2,4,4,2,8,128]{5,4,3,2,1,0:T(8,128)} %bitcast.11, f32[8,128]{1,0:T(8,128)} %get-tuple-element.9.total_ref, s32[1,1,256]{2,1,0:T(1,128)} %counts_ref.1), custom_call_target="tpu_custom_call" | custom-call | tf_op jit(solution)/shard_map/reduce_rows/pallas_call | solution.py:344
  70.8 43.6 %fourier.1 = f32[2,8,4,1024]{3,2,1,0:T(4,128)} custom-call(f32[8,48,128]{2,1,0:T(8,128)} %get-tuple-element.10.pack_ref, f32[2,8,128]{2,1,0:T(8,128)} %constant.30.clone.twist_y, bf16[256,256]{1,0:T(8,128)(2,1)} %constant.31.clone.y_high, bf16[256,256]{1,0:T(8,128)(2,1)} %constant.32.clone.y_low, bf16[256,512]{1,0:T(8,128)(2,1)} %constant.33.clone.x_both, ...), custom_call_target="tpu_custom_call" | custom-call | tf_op jit(solution)/shard_map/fourier/pallas_call | solution.py:556
  114.4 1.7 %copy.17 = f32[2,8,4,1024]{3,2,1,0:T(4,128)} copy(f32[2,8,4,1024]{3,2,1,0:T(4,128)} %fourier.1) | data formatting | bytes 524288
  116.1 1.2 %copy.18 = s32[1,1,256]{2,1,0:T(1,128)} copy(s32[1,1,256]{2,1,0:T(1,128)} %get-tuple-element.15) | data formatting | bytes 2048

commit v3 on v1

v3 whole, which is shorter than its diff:
```python
import functools
import math

import jax
import jax.numpy as jnp
import numpy as np
from jax import lax
from jax.experimental import pallas as pl
from jax.experimental.pallas import tpu as pltpu
from jax.sharding import Mesh
from jax.sharding import PartitionSpec as P

NX = 1024
NY = 1024
PLANES = 8
BETA = 18.4
OWNERS = 32
RX = 32
TILE = 128
NT = (((1,), (1,)), ((), ()))


def tap_values(step, fraction):
    z = (step.astype(jnp.float32) - fraction) * 0.25
    return jnp.exp(BETA * (jnp.sqrt(1.0 - z * z) - 1.0))


def spread_kernel(
    owner_ref, cell_ref, fx_ref, fy_ref, mass_ref, live_ref,
    main_ref, rim_ref, total_ref,
    grid_acc, rim_acc, lx_s, ly_s, fx_s, fy_s, w_s,
):
    tiles = cell_ref.shape[0]
    zero = jnp.zeros((8, TILE), jnp.float32)

    def clear(i, _):
        for p in range(PLANES):
            grid_acc[p, pl.ds(pl.multiple_of(i * 8, 8), 8), :] = zero
        return 0

    lax.fori_loop(0, grid_acc.shape[1] // 8, clear, 0)

    def clear_rim(i, _):
        for p in range(8):
            rim_acc[i * 8 + p] = zero
        return 0

    lax.fori_loop(0, OWNERS, clear_rim, 0)

    def prepare(i, _):
        rows = pl.ds(pl.multiple_of(i * 16, 16), 16)
        cell = cell_ref[rows, :]
        ly_s[rows, :] = cell & 127
        lx_s[rows, :] = (cell >> 7) & 31
        fx_s[rows, :] = fx_ref[rows, :].astype(jnp.float32)
        fy_s[rows, :] = fy_ref[rows, :].astype(jnp.float32)
        w_s[rows, :] = jnp.where(live_ref[rows, :] == 1, mass_ref[rows, :].astype(jnp.float32), 0.0)
        return 0

    lax.fori_loop(0, tiles // 16, prepare, 0)

    sub = lax.broadcasted_iota(jnp.int32, (8, TILE), 0)

    def row(ref, t):
        return jnp.broadcast_to(ref[pl.ds(t, 1), :], (8, TILE))

    def one_tile(t):
        lx, ly = row(lx_s, t), row(ly_s, t)
        jx = (sub - lx + 3) & 7
        jy = (sub - ly + 3) & 7
        tx = tap_values(jx - 3, row(fx_s, t))
        ty = tap_values(jy - 3, row(fy_s, t)) * row(w_s, t)
        gx = (lx + jx + 5) >> 3
        gy = (ly + jy - 3) >> 3
        gy = jnp.where(gy < 0, 16, gy)
        wx = jnp.concatenate([jnp.where(gx == g, tx, 0.0) for g in range(6)]).astype(jnp.bfloat16)
        wy = jnp.concatenate([jnp.where(gy == g, ty, 0.0) for g in range(16)]).astype(jnp.bfloat16)
        wr = jnp.concatenate([jnp.where(gy == 16, ty, 0.0), zero]).astype(jnp.bfloat16)
        main = lax.dot_general(wx, wy, NT, preferred_element_type=jnp.float32)
        rim = lax.dot_general(wr, wx, NT, preferred_element_type=jnp.float32)
        return main, rim[:8]

    unroll = 32

    def add_tiles(i, _):
        results = [one_tile(i * unroll + k) for k in range(unroll)]
        for k in range(unroll):
            owner = owner_ref[0, i * unroll + k]
            plane = cell_ref[pl.ds(i * unroll + k, 1), :][0, 0] >> 12
            bucket = owner * 8 + plane
            main, rim = results[k]
            rows = pl.ds(pl.multiple_of(owner * RX, RX), 48)
            grid_acc[plane, rows, :] = grid_acc[plane, rows, :] + main
            rim_acc[bucket, :, :48] = rim_acc[bucket, :, :48] + rim
        return 0

    lax.fori_loop(0, tiles // unroll, add_tiles, 0)

    for p in range(PLANES):
        grid_acc[p, 1024:1032, :] = grid_acc[p, 1024:1032, :] + grid_acc[p, 0:8, :]
        grid_acc[p, 8:16, :] = grid_acc[p, 8:16, :] + grid_acc[p, 1032:1040, :]

    lane = lax.broadcasted_iota(jnp.int32, (8, TILE), 1)

    def write_out(i, total):
        rows = pl.ds(pl.multiple_of(i * RX + 8, 8), RX)
        for p in range(PLANES):
            block = grid_acc[p, rows, :]
            main_ref[p, i // 2, i % 2] = block
            for k in range(RX // 8):
                total = total + block[8 * k : 8 * k + 8, :]
        before, after = (i + OWNERS - 1) % OWNERS, (i + 1) % OWNERS
        for q in range(2):
            out = zero
            for k in range(4):
                p = 4 * q + k
                own = pltpu.roll(rim_acc[i * 8 + p], (32 * k - 8) % 128, 1)
                low = pltpu.roll(rim_acc[before * 8 + p], (32 * k - 40) % 128, 1)
                high = pltpu.roll(rim_acc[after * 8 + p], (32 * k + 24) % 128, 1)
                spot = lane - 32 * k
                out = jnp.where((spot >= 0) & (spot < 32), own, out)
                out = out + jnp.where((spot >= 0) & (spot < 8), low, 0.0)
                out = out + jnp.where((spot >= 24) & (spot < 32), high, 0.0)
            rim_ref[q, i // 2, i % 2] = out
            total = total + out
        return total

    total_ref[...] = lax.fori_loop(0, OWNERS, write_out, zero)


def spread(owners, cells, fx, fy, mass, live):
    tiles = cells.shape[0]
    vmem = pl.BlockSpec(memory_space=pltpu.VMEM)
    return pl.pallas_call(
        spread_kernel,
        out_shape=(
            jax.ShapeDtypeStruct((PLANES, 16, 2, RX, TILE), jnp.float32),
            jax.ShapeDtypeStruct((2, 16, 2, 8, TILE), jnp.float32),
            jax.ShapeDtypeStruct((8, TILE), jnp.float32),
        ),
        in_specs=[pl.BlockSpec(memory_space=pltpu.SMEM)] + [vmem] * 5,
        out_specs=(vmem, vmem, vmem),
        scratch_shapes=[
            pltpu.VMEM((PLANES, NX + 16, TILE), jnp.float32),
            pltpu.VMEM((OWNERS * PLANES, 8, TILE), jnp.float32),
            pltpu.VMEM((tiles, TILE), jnp.int32),
            pltpu.VMEM((tiles, TILE), jnp.int32),
            pltpu.VMEM((tiles, TILE), jnp.float32),
            pltpu.VMEM((tiles, TILE), jnp.float32),
            pltpu.VMEM((tiles, TILE), jnp.float32),
        ],
        compiler_params=pltpu.CompilerParams(vmem_limit_bytes=24 << 20),
        name="spread",
    )(owners, cells, fx, fy, mass, live)


COORDS = ("px_0", "px_1", "px_2")
DEVICES = 256


def split_bf16(value):
    high = value.astype(jnp.bfloat16)
    return high, (value - high.astype(jnp.float32)).astype(jnp.bfloat16)


def np_split(value):
    high = np.asarray(value, np.float32).astype(jnp.bfloat16)
    low = (np.asarray(value, np.float64) - high.astype(np.float64)).astype(jnp.bfloat16)
    return high, low


def tables():
    k = np.arange(TILE)
    turn_y = 2 * np.pi / NY * (np.arange(8)[:, None] * k[None, :])
    twist_y = np.stack([np.cos(turn_y), -np.sin(turn_y)]).astype(np.float32)
    theta = 2 * np.pi / TILE * (k[:, None] * k[None, :] % TILE)
    wave_y = np.zeros((TILE, 2, 2, TILE))
    wave_y[:, 0, 0], wave_y[:, 0, 1] = np.cos(theta), np.sin(theta)
    wave_y[:, 1, 0], wave_y[:, 1, 1] = -np.sin(theta), np.cos(theta)
    y_high, y_low = np_split(wave_y.reshape(2 * TILE, 2 * TILE))
    phase = 2 * np.pi / OWNERS * (np.arange(OWNERS)[:, None] * k[None, :] % OWNERS)
    block = np.zeros((OWNERS, 2, 2, TILE))
    block[:, 0, 0], block[:, 1, 0] = np.cos(phase), np.sin(phase)
    block[:, 0, 1], block[:, 1, 1] = -np.sin(phase), np.cos(phase)
    wave_x = np.kron(np.eye(2), block.reshape(2 * OWNERS, 2 * TILE))
    x_high, x_low = np_split(wave_x)
    turn_x = 2 * np.pi / NX * (np.arange(RX)[:, None] * k[None, :])
    scale = 1.0 / math.sqrt(NX * NY)
    twist_x = (scale * np.stack([np.cos(turn_x), -np.sin(turn_x)])).astype(np.float32)
    return (twist_y, y_high, y_low), (np.concatenate([x_high, x_high]), x_low, twist_x)


HALF = math.sqrt(0.5)


def real_eighths(d):
    s = [d[k] + d[k + 4] for k in range(4)]
    e = [d[k] - d[k + 4] for k in range(4)]
    near_sum, far_sum = s[0] + s[2], s[1] + s[3]
    a0, a4 = near_sum + far_sum, near_sum - far_sum
    re2, im2 = s[0] - s[2], s[3] - s[1]
    tilt, lean = (e[1] - e[3]) * HALF, (e[1] + e[3]) * HALF
    re1, im1 = e[0] + tilt, -e[2] - lean
    re3, im3 = e[0] - tilt, e[2] - lean
    zero = jnp.zeros_like(a0)
    return [(a0, zero), (re1, im1), (re2, im2), (re3, im3), (a4, zero), (re3, -im3), (re2, -im2), (re1, -im1)]


def fourths(t):
    def add(p, q):
        return p[0] + q[0], p[1] + q[1]

    def less(p, q):
        return p[0] - q[0], p[1] - q[1]

    e0, e1 = add(t[0], t[2]), less(t[0], t[2])
    f0, g = add(t[1], t[3]), less(t[1], t[3])
    f1 = (g[1], -g[0])
    return [add(e0, f0), add(e1, f1), less(e0, f0), less(e1, f1)]


def eighths(z):
    s = [(z[k][0] + z[k + 4][0], z[k][1] + z[k + 4][1]) for k in range(4)]
    d = [(z[k][0] - z[k + 4][0], z[k][1] - z[k + 4][1]) for k in range(4)]
    turned = [
        d[0],
        ((d[1][0] + d[1][1]) * HALF, (d[1][1] - d[1][0]) * HALF),
        (d[2][1], -d[2][0]),
        ((d[3][1] - d[3][0]) * HALF, -(d[3][0] + d[3][1]) * HALF),
    ]
    even, odd = fourths(s), fourths(turned)
    return [even[0], odd[0], even[1], odd[1], even[2], odd[2], even[3], odd[3]]


def near(v):
    return v + 1 - 2 * lax.rem(v, 2)


def far(v):
    return 3 - v


ROUTES = (("x", "near"), ("x", "far"), ("y", "near"), ("y", "far"))
MESH = pl.DeviceIdType.MESH


def place(index):
    row = index // 8
    return {"px_0": row // 8, "px_1": lax.rem(row // 2, 4), "px_2": lax.rem(row, 2), "py": lax.rem(index, 8)}


def transform_kernel(
    main_ref, rim_ref, total_ref, counts_ref, twist_y, y_high, y_low,
    columns, begin_out,
    main0, rim0, main1, rim1, main2, rim2, main3, rim3, main4, rim4,
    note, notes, pack, got, waves,
    note_send, note_recv, send, recv, py_send, py_recv, wave_send, wave_recv,
):
    x, y, c = (lax.axis_index(a) for a in COORDS)
    j = lax.axis_index("py")
    i = (x * 4 + y) * 2 + c
    me = i * 8 + j
    barrier = pltpu.get_barrier_semaphore()

    def device(x, y, c):
        return ((x * 4 + y) * 2 + c) * 8 + j

    for k in range(1, OWNERS):
        pl.semaphore_signal(barrier, inc=1, device_id=place(lax.rem(me + 8 * k, DEVICES)), device_id_type=MESH)
    for k in range(1, 8):
        pl.semaphore_signal(barrier, inc=1, device_id=place(i * 8 + lax.rem(j + k, 8)), device_id_type=MESH)
    note[0:1, :] = counts_ref[0, :, 0:TILE].astype(jnp.float32)
    note[1:2, :] = counts_ref[0, :, TILE:].astype(jnp.float32)
    note[2:3, :] = jnp.sum(total_ref[...], axis=0, keepdims=True)
    note[3:8, :] = jnp.zeros((5, TILE), jnp.float32)
    notes[i] = note[...]
    pl.semaphore_wait(barrier, OWNERS - 1 + 7)

    def remote(src, dst, slot, where):
        copy = pltpu.make_async_remote_copy(
            src_ref=src, dst_ref=dst, send_sem=send.at[slot], recv_sem=recv.at[slot],
            device_id=place(where), device_id_type=MESH,
        )
        copy.start()
        return copy

    chunks = {}
    for k in (8, 9, *range(8)):
        if k < 8:
            refs = (main_ref.at[k], *(r.at[k] for r in (main0, main1, main2, main3, main4)))
        else:
            refs = (rim_ref.at[k - 8], *(r.at[k - 8] for r in (rim0, rim1, rim2, rim3, rim4)))
        chunks[k] = (*refs, k % 4 if k < 8 else 2 * (k - 8))

    def leg(first, kind):
        v = x if first == "x" else y
        if kind == "near":
            low = lax.rem((v + 1) // 2, 2)
            keep, give = (low, 3 - low), (1 - low, 2 + low)
            partner, other = near(v), far(v)
        else:
            low = 2 * (v // 2)
            keep, give = (low, low + 1), (2 - low, 3 - low)
            partner, other = far(v), near(v)
        if first == "x":
            return keep, give, device(partner, y, c), other, device(other, y, c)
        return keep, give, device(x, partner, c), other, device(x, other, c)

    pending = {}
    for k, (src, b0, *_) in chunks.items():
        pending[k] = [remote(src.at[:, :, 1 - c], b0, 7 * k, device(x, y, 1 - c))]

    def note_copy(k):
        peer = lax.rem(i + k, OWNERS)
        return pltpu.make_async_remote_copy(
            src_ref=note, dst_ref=notes.at[i], send_sem=note_send.at[peer], recv_sem=note_recv.at[i],
            device_id=place(peer * 8 + j), device_id_type=MESH,
        )

    for k in range(1, OWNERS):
        note_copy(k).start()
    sent = []

    def arrive(k):
        for copy in pending[k]:
            copy.wait_recv()
        sent.extend(pending[k])

    for k, (src, b0, b1, b2, b3, b4, route) in chunks.items():
        arrive(k)

        def add0(n, _, src=src, b0=b0):
            for m in range(4):
                b0[n, m] = b0[n, m] + src[n, m, c]
            return 0

        lax.fori_loop(0, 4, add0, 0)
        first, kind = ROUTES[route]
        _, give, where, _, _ = leg(first, kind)
        pending[k] = []
        for n in range(2):
            block = b0.at[give[n]] if first == "x" else b0.at[:, give[n]]
            pending[k].append(remote(block, b1.at[n], 7 * k + 1 + n, where))

    for k, (src, b0, b1, b2, b3, b4, route) in chunks.items():
        arrive(k)
        first, kind = ROUTES[route]
        keep, _, _, other, where = leg(first, kind)
        for n in range(2):
            for m in range(4):
                at = (keep[n], m) if first == "x" else (m, keep[n])
                b0[at] = b0[at] + b1[n, m]
        block = b0.at[other] if first == "x" else b0.at[:, other]
        pending[k] = [remote(block, b2, 7 * k + 3, where)]

    for k, (src, b0, b1, b2, b3, b4, route) in chunks.items():
        arrive(k)
        first, kind = ROUTES[route]
        for m in range(4):
            at = (x, m) if first == "x" else (m, y)
            b0[at] = b0[at] + b2[m]
        second = "y" if first == "x" else "x"
        _, give, where, _, _ = leg(second, kind)
        pending[k] = []
        for n in range(2):
            block = b0.at[x, give[n]] if first == "x" else b0.at[give[n], y]
            pending[k].append(remote(block, b3.at[n], 7 * k + 4 + n, where))

    for k, (src, b0, b1, b2, b3, b4, route) in chunks.items():
        arrive(k)
        first, kind = ROUTES[route]
        second = "y" if first == "x" else "x"
        keep, _, _, other, where = leg(second, kind)
        for n in range(2):
            at = (x, keep[n]) if first == "x" else (keep[n], y)
            b0[at] = b0[at] + b3[n]
        block = b0.at[x, other] if first == "x" else b0.at[other, y]
        pending[k] = [remote(block, b4, 7 * k + 6, where)]

    for k in range(1, OWNERS):
        peer = lax.rem(i + k, OWNERS)
        copy = pltpu.make_async_remote_copy(
            src_ref=note, dst_ref=notes.at[peer], send_sem=note_send.at[peer], recv_sem=note_recv.at[peer],
            device_id=place(peer * 8 + j), device_id_type=MESH,
        )
        copy.wait_send()
        copy.wait_recv()
    everyone = notes[0]
    for k in range(1, OWNERS):
        everyone = everyone + notes[k]
    amount = jnp.broadcast_to(everyone[2:3, :], (8, TILE))

    def plane_copy(k, source):
        return pltpu.make_async_remote_copy(
            src_ref=pack.at[k], dst_ref=got.at[source], send_sem=py_send.at[k], recv_sem=py_recv.at[source],
            device_id=place(i * 8 + k), device_id_type=MESH,
        )

    for k, (src, b0, b1, b2, b3, b4, route) in chunks.items():
        arrive(k)
        block = b0[x, y] + b4[...]
        if k >= 8:
            for p in range(4):
                pack[4 * (k - 8) + p, RX : RX + 8, :] = block
                pack[4 * (k - 8) + p, RX + 8 :, :] = amount
            continue
        pack[k, 0:RX, :] = block

        @pl.when(k != j)
        def _():
            plane_copy(k, j).start()

        @pl.when(k == j)
        def _():
            got[k] = pack[k]

    earlier = jnp.zeros((8, TILE), jnp.float32)
    for k in range(OWNERS):
        earlier = earlier + jnp.where(k < i, notes[k], 0.0)
    spot = lax.broadcasted_iota(jnp.int32, (8, TILE), 1)
    running = everyone
    for shift in (1, 2, 4, 8, 16, 32, 64):
        running = running + jnp.where(spot >= shift, pltpu.roll(running, shift, 1), 0.0)
    begin = running - everyone + earlier
    whole = jnp.sum(everyone[0:1, :], axis=1, keepdims=True)
    begin_out[0:1, :] = begin[0:1, :]
    begin_out[1:2, :] = begin[1:2, :] + whole
    begin_out[2:8, :] = jnp.zeros((6, TILE), jnp.float32)

    for k in range(1, 8):
        peer = lax.rem(j + k, 8)
        plane_copy(peer, j).wait_send()
        plane_copy(peer, peer).wait_recv()

    lane = lax.broadcasted_iota(jnp.int32, (RX, TILE), 1)
    rims = jnp.concatenate([got[s, 32:40, :] for s in range(8)])
    rims = pltpu.roll(rims, (TILE - 32 * (j % 4)) % TILE, 1)
    rims = jnp.concatenate([rims, jnp.zeros((64, TILE), jnp.float32)])
    rims = jnp.transpose(rims)[:RX]
    mass_sum = got[0, 40:41, :]
    for s in range(1, 8):
        mass_sum = mass_sum + got[s, 40:41, :]
    inverse = float(PLANES * NX * NY) / jnp.sum(mass_sum, axis=1, keepdims=True)
    blocks = []
    for s in range(8):
        right = pltpu.roll(rims, (-8 * ((s + 7) % 8)) % TILE, 1)
        left = pltpu.roll(rims, (120 - 8 * ((s + 1) % 8)) % TILE, 1)
        value = got[s, 0:32, :] + jnp.where(lane < 4, right, 0.0) + jnp.where(lane >= 125, left, 0.0)
        blocks.append(value * inverse - 1.0)
    turned = []
    for k, (re, im) in enumerate(real_eighths(blocks)):
        tr, ti = twist_y[0, k : k + 1, :], twist_y[1, k : k + 1, :]
        turned.append(jnp.concatenate([re * tr - im * ti, re * ti + im * tr], axis=1))
    high, low = split_bf16(jnp.concatenate(turned))

    def times(a, b):
        return lax.dot_general(a, b, NT, preferred_element_type=jnp.float32)

    wave = times(y_high[...], low) + times(y_low[...], high) + times(y_high[...], high)
    for h in range(2):
        for k in range(TILE):
            waves[2 * k + h] = wave[2 * k : 2 * k + 2, TILE * h : TILE * h + TILE]

    columns[j * 32 + i] = waves[me]

    def hand_out(k, _):
        for n in range(5):
            peer = lax.rem(me + 5 * k + n + 1, DEVICES)
            pltpu.make_async_remote_copy(
                src_ref=waves.at[peer], dst_ref=columns.at[j * 32 + i],
                send_sem=wave_send, recv_sem=wave_recv,
                device_id=place(peer), device_id_type=MESH,
            ).start()
        return 0

    lax.fori_loop(0, (DEVICES - 1) // 5, hand_out, 0)
    for copy in sent:
        copy.wait_send()
    others = columns.at[pl.ds(0, DEVICES - 1)]
    pltpu.make_async_copy(others, others, wave_recv).wait()
    pltpu.make_async_copy(others, others, wave_send).wait()


def transform(main, rim, total, counts, wave_tables):
    vmem = pl.BlockSpec(memory_space=pltpu.VMEM)
    f32 = jnp.float32

    def both(*lead):
        return [pltpu.VMEM((PLANES, *lead, RX, TILE), f32), pltpu.VMEM((2, *lead, 8, TILE), f32)]

    dma = pltpu.SemaphoreType.DMA
    return pl.pallas_call(
        transform_kernel,
        out_shape=(
            jax.ShapeDtypeStruct((DEVICES, 2, TILE), f32),
            jax.ShapeDtypeStruct((8, TILE), f32),
        ),
        in_specs=[vmem] * 7,
        out_specs=(vmem, vmem),
        scratch_shapes=[
            *both(4, 4), *both(2, 4), *both(4), *both(2), *both(),
            pltpu.VMEM((8, TILE), f32),
            pltpu.VMEM((OWNERS, 8, TILE), f32),
            pltpu.VMEM((PLANES, RX + 16, TILE), f32),
            pltpu.VMEM((PLANES, RX + 16, TILE), f32),
            pltpu.VMEM((DEVICES, 2, TILE), f32),
            dma((OWNERS,)), dma((OWNERS,)), dma((70,)), dma((70,)), dma((8,)), dma((8,)), dma, dma,
        ],
        compiler_params=pltpu.CompilerParams(
            collective_id=0, has_side_effects=True, vmem_limit_bytes=24 << 20
        ),
        name="transform",
    )(main, rim, total, counts, *wave_tables)


def finish_kernel(columns, begin_ref, x_both, x_low, twist_x, out_ref, start_ref):
    start_ref[0, :, 0:TILE] = begin_ref[0:1, :].astype(jnp.int32)
    start_ref[0, :, TILE:] = begin_ref[1:2, :].astype(jnp.int32)
    for g in range(4):
        pair = columns[64 * g : 64 * g + 64].reshape(TILE, TILE)
        high, low = split_bf16(jnp.transpose(pair))
        both = jnp.concatenate([high, low], axis=1)
        sums = jnp.dot(both, x_both[...], preferred_element_type=jnp.float32)
        sums = sums + jnp.dot(high, x_low[...], preferred_element_type=jnp.float32)
        parts = [[], []]
        for p in range(2):
            for w in range(4):
                re_sum = im_sum = None
                for q in range(4):
                    rows = slice(32 * w + 8 * q, 32 * w + 8 * q + 8)
                    re = sums[rows, 256 * p : 256 * p + 128]
                    im = sums[rows, 256 * p + 128 : 256 * p + 256]
                    tr, ti = twist_x[0, 8 * q : 8 * q + 8, :], twist_x[1, 8 * q : 8 * q + 8, :]
                    re_part, im_part = re * tr - im * ti, re * ti + im * tr
                    re_sum = re_part if q == 0 else re_sum + re_part
                    im_sum = im_part if q == 0 else im_sum + im_part
                parts[0].append(re_sum)
                parts[1].append(im_sum)
        re, im = (jnp.transpose(jnp.stack(part), (1, 0, 2)) for part in parts)
        for a, value in enumerate(eighths([(re[k], im[k]) for k in range(8)])):
            for n in range(2):
                for p in range(2):
                    out_ref[n, 2 * g + p, :, TILE * a : TILE * a + TILE] = value[n][4 * p : 4 * p + 4]


def finish(columns, begin, wave_tables):
    vmem = pl.BlockSpec(memory_space=pltpu.VMEM)
    return pl.pallas_call(
        finish_kernel,
        out_shape=(
            jax.ShapeDtypeStruct((2, PLANES, 4, NX), jnp.float32),
            jax.ShapeDtypeStruct((1, 1, 2 * TILE), jnp.int32),
        ),
        in_specs=[vmem] * 5,
        out_specs=(vmem, vmem),
        compiler_params=pltpu.CompilerParams(vmem_limit_bytes=24 << 20),
        name="finish",
    )(columns, begin, *wave_tables)


PX = ("px_0", "px_1", "px_2")
PX_PY = ("px_0", "px_1", "px_2", "py")


def local(cell_ids, offset_x, offset_y, mass, live, tile_owner, counts):
    main, rim, total = spread(tile_owner, cell_ids[0], offset_x[0], offset_y[0], mass[0], live[0])
    y_tables, x_tables = tables()
    columns, begin = transform(
        main.reshape(PLANES, 4, 4, 2, RX, TILE), rim.reshape(2, 4, 4, 2, 8, TILE), total, counts, y_tables
    )
    return finish(columns, begin, x_tables)


def solution(mesh):
    torus = Mesh(mesh.devices.reshape(4, 4, 2, mesh.shape["py"]), ("px_0", "px_1", "px_2", "py"))
    return jax.shard_map(
        local,
        mesh=torus,
        in_specs=(
            P(PX, "py", None),
            P(PX, "py", None),
            P(PX, "py", None),
            P(PX, "py", None),
            P(PX, "py", None),
            P(PX, "py"),
            P(PX, "py", None),
        ),
        out_specs=(P(None, None, PX_PY, None), P(PX, "py", None)),
        check_vma=False,
    )
```

time: 296 us -> 87.6 us (0.30); the launches traced: 291 us -> 87.2 us
  matrix products: 103 us -> 0 us
  starting transfers between devices: 42.5 us -> 0 us
  local copies, waits for them, and re-layouts: 34.9 us -> 8.56 us
  other arithmetic: 24.9 us -> 0 us
  blocking collectives: 13.1 us -> 0 us
  Pallas kernels: 67.7 us -> 77.9 us
  waiting for transfers between devices: 3.68 us -> 0 us
    dot_general x6 -> x0, matrix products: 103 us -> none  [the longest x4 73.4 us: project(): jnp.einsum('pqy,qk->pyk', data_block, table, precision=lax.Precision.HIGH...]
    all_to_all x3 -> x0, starting transfers between devices: 36.7 us -> none  [the longest x2 32.7 us: one_exchange(): parts = lax.all_to_all(parts, axis, split_axis=0, concat_axis=0, tiled=True)]
    pallas_call x1 -> x2, Pallas kernels: 30.2 us -> 51.4 us  [the longest x1 50.2 us: transform(): pl.pallas_call(transform_kernel, out_shape=(jax.ShapeDtypeStruct((DEVICES...]
    cos x1 -> x0, other arithmetic: 17.5 us -> none  [local(): jnp.cos(angle_y)]
    psum x1 -> x0, blocking collectives: 13.1 us -> none  [local(): grand_total = lax.psum(jnp.sum(total[0]), 'py')]
    pallas_call x1, Pallas kernels: 37.5 us -> 26.5 us  [spread(): pl.pallas_call(spread_kernel, out_shape=(jax.ShapeDtypeStruct((PLANES, 16...]
    transpose x6 -> x0, local copies, waits for them, and re-layouts: 10.1 us -> none  [the longest x4 9.75 us: laid_out(): return jnp.moveaxis(parts, 0, dim).reshape(lengths)]
    reshape x5 -> x0, local copies, waits for them, and re-layouts: 5.81 us -> none  [the longest x2 4.63 us: one_exchange(): parts = parts.reshape(-1, *inside)]
  transfers between devices with their start and end apart: 5 -> 0, of which waited for: 1 -> 0; matrix products, arithmetic and copies ran while one was open for 16% -> 0% of each run, Pallas kernels for 0% -> 0%
where the time goes in v3:
time: 87.6 us; the launch traced here: 87.2 us
  Pallas kernels  77.9 us (89%)
  local copies, waits for them, and re-layouts  8.56 us (10%)
    pallas_call x1, Pallas kernels, transform(): pl.pallas_call(transform_kernel, out_shape=(jax.ShapeDtypeStruct((DEVICES...  50.2 us
    pallas_call x1, Pallas kernels, spread(): pl.pallas_call(spread_kernel, out_shape=(jax.ShapeDtypeStruct((PLANES, 16...  26.5 us
    unnamed x26, local copies, waits for them, and re-layouts  8.56 us

profile of v3, /device:TPU:1, one launch (start us, length us, event | category | flops | bytes accessed | tf_op | source)
XLA Modules:
  0.0 87.2 jit_solution(4022625776812879259)
XLA Ops:
  0.6 0.0 copy-start
  0.6 1.0 %copy-done = s32[1,640,128]{2,1,0:T(8,128)S(1)} copy-done((s32[1,640,128]{2,1,0:T(8,128)S(1)}, s32[1,640,128]{2,1,0:T(8,128)}, u32[]{:S(2)}) %copy-start) | copy-done | bytes 327704
  1.6 0.0 copy-start.1
  1.6 1.0 %copy-done.1 = s32[1,640,128]{2,1,0:T(8,128)S(1)} copy-done((s32[1,640,128]{2,1,0:T(8,128)S(1)}, s32[1,640,128]{2,1,0:T(8,128)}, u32[]{:S(2)}) %copy-start.1) | copy-done | bytes 327704
  2.6 0.0 copy-start.3
  2.6 0.9 %copy-done.3 = bf16[1,640,128]{2,1,0:T(8,128)(2,1)S(1)} copy-done((bf16[1,640,128]{2,1,0:T(8,128)(2,1)S(1)}, bf16[1,640,128]{2,1,0:T(8,128)(2,1)}, u32[]{:S(2)}) %copy-start.3) | copy-done | bytes 163864
  3.5 0.0 copy-start.4
  3.5 0.9 %copy-done.4 = bf16[1,640,128]{2,1,0:T(8,128)(2,1)S(1)} copy-done((bf16[1,640,128]{2,1,0:T(8,128)(2,1)S(1)}, bf16[1,640,128]{2,1,0:T(8,128)(2,1)}, u32[]{:S(2)}) %copy-start.4) | copy-done | bytes 163864
  4.4 0.0 copy-start.5
  4.4 0.9 %copy-done.5 = bf16[1,640,128]{2,1,0:T(8,128)(2,1)S(1)} copy-done((bf16[1,640,128]{2,1,0:T(8,128)(2,1)S(1)}, bf16[1,640,128]{2,1,0:T(8,128)(2,1)}, u32[]{:S(2)}) %copy-start.5) | copy-done | bytes 163864
  5.3 0.0 copy-start.11
  5.3 0.7 copy-done.11
  6.0 0.0 copy-start.2
  6.0 26.5 %spread.1 = (f32[8,16,2,32,128]{4,3,2,1,0:T(8,128)S(1)}, f32[2,16,2,8,128]{4,3,2,1,0:T(8,128)S(1)}, f32[8,128]{1,0:T(8,128)S(1)}) custom-call(s32[1,640]{1,0:T(1,128)S(1)} %copy-done.11, s32[640,128]{1,0:T(8,128)S(1)} %bitcast.8, bf16[640,128]{1,0:T(8,128)(2,1)S(1)} %bitcast.11, bf16[640,128]{1,0:T(8,128)(2,1)S(1)} %bitcast.12, ...), custom_call_target="tpu_custom_call" | custom-call | tf_op jit(solution)/shard_map/spread/pallas_call | solution.py:134
  32.6 0.0 copy-start.6
  32.6 0.9 %copy-done.6 = bf16[256,256]{1,0:T(8,128)(2,1)S(1)} copy-done((bf16[256,256]{1,0:T(8,128)(2,1)S(1)}, bf16[256,256]{1,0:T(8,128)(2,1)}, u32[]{:S(2)}) %copy-start.6) | copy-done | bytes 131096
  33.5 0.9 %copy-done.7 = bf16[256,256]{1,0:T(8,128)(2,1)S(1)} copy-done((bf16[256,256]{1,0:T(8,128)(2,1)S(1)}, bf16[256,256]{1,0:T(8,128)(2,1)}, u32[]{:S(2)}) %copy-start.7) | copy-done | bytes 131096
  34.4 0.7 copy-done.10
  35.1 0.7 copy-done.12
  35.7 50.2 %transform.1 = (f32[256,2,128]{2,1,0:T(2,128)S(1)}, f32[8,128]{1,0:T(8,128)S(1)}) custom-call(f32[8,4,4,2,32,128]{5,4,3,2,1,0:T(8,128)S(1)} %bitcast.7, f32[2,4,4,2,8,128]{5,4,3,2,1,0:T(8,128)S(1)} %bitcast.10, f32[8,128]{1,0:T(8,128)S(1)} %get-tuple-element.9.total_ref, s32[1,1,256]{2,1,0:T(1,128)S(1)} %copy-done.12, f32[2,8,128]{2,1,0:T(8,128)S(1)} %copy-done.10, ...), custom_call_target="tpu_custom_call" | custom-call | tf_op jit(solution)/shard_map/transform/pallas_call | solution.py:492
  85.9 0.0 copy-done.2
  85.9 0.0 copy-done.8
  86.0 0.0 copy-done.9
  86.0 1.2 %finish.1 = (f32[2,8,4,1024]{3,2,1,0:T(4,128)}, s32[1,1,256]{2,1,0:T(1,128)}) custom-call(f32[256,2,128]{2,1,0:T(2,128)S(1)} %get-tuple-element.10.columns, f32[8,128]{1,0:T(8,128)S(1)} %get-tuple-element.11.begin_ref, bf16[256,512]{1,0:T(8,128)(2,1)S(1)} %copy-done.2, bf16[128,512]{1,0:T(8,128)(2,1)S(1)} %copy-done.8, f32[2,32,128]{2,1,0:T(8,128)S(1)} %copy-done.9), custom_call_target="tpu_custom_call" | custom-call | tf_op jit(solution)/shard_map/finish/pallas_call | solution.py:548
  (5 shorter events, 0.0 us)
Async XLA Ops:
  0.6 1.0 %copy-start = (s32[1,640,128]{2,1,0:T(8,128)S(1)}, s32[1,640,128]{2,1,0:T(8,128)}, u32[]{:S(2)}) copy-start(s32[1,640,128]{2,1,0:T(8,128)} %param.13) | copy-start | bytes 983044
  1.6 1.0 %copy-start.1 = (s32[1,640,128]{2,1,0:T(8,128)S(1)}, s32[1,640,128]{2,1,0:T(8,128)}, u32[]{:S(2)}) copy-start(s32[1,640,128]{2,1,0:T(8,128)} %param.17) | copy-start | bytes 983044
  2.6 0.9 %copy-start.3 = (bf16[1,640,128]{2,1,0:T(8,128)(2,1)S(1)}, bf16[1,640,128]{2,1,0:T(8,128)(2,1)}, u32[]{:S(2)}) copy-start(bf16[1,640,128]{2,1,0:T(8,128)(2,1)} %param.14) | copy-start | bytes 491524
  3.5 0.9 %copy-start.4 = (bf16[1,640,128]{2,1,0:T(8,128)(2,1)S(1)}, bf16[1,640,128]{2,1,0:T(8,128)(2,1)}, u32[]{:S(2)}) copy-start(bf16[1,640,128]{2,1,0:T(8,128)(2,1)} %param.15) | copy-start | bytes 491524
  4.4 0.9 %copy-start.5 = (bf16[1,640,128]{2,1,0:T(8,128)(2,1)S(1)}, bf16[1,640,128]{2,1,0:T(8,128)(2,1)}, u32[]{:S(2)}) copy-start(bf16[1,640,128]{2,1,0:T(8,128)(2,1)} %param.16) | copy-start | bytes 491524
  5.3 0.7 copy-start.11
  6.0 79.9 %copy-start.2 = (bf16[256,512]{1,0:T(8,128)(2,1)S(1)}, bf16[256,512]{1,0:T(8,128)(2,1)}, u32[]{:S(2)}) copy-start(bf16[256,512]{1,0:T(8,128)(2,1)} %constant.15.clone.x_both) | copy-start | bytes 786436
  6.0 79.9 %copy-start.8 = (bf16[128,512]{1,0:T(8,128)(2,1)S(1)}, bf16[128,512]{1,0:T(8,128)(2,1)}, u32[]{:S(2)}) copy-start(bf16[128,512]{1,0:T(8,128)(2,1)} %constant.16.clone.x_low) | copy-start | bytes 393220
  6.0 79.9 %copy-start.9 = (f32[2,32,128]{2,1,0:T(8,128)S(1)}, f32[2,32,128]{2,1,0:T(8,128)}, u32[]{:S(2)}) copy-start(f32[2,32,128]{2,1,0:T(8,128)} %constant.17.clone.twist_x) | copy-start | bytes 98308
  32.6 0.9 %copy-start.6 = (bf16[256,256]{1,0:T(8,128)(2,1)S(1)}, bf16[256,256]{1,0:T(8,128)(2,1)}, u32[]{:S(2)}) copy-start(bf16[256,256]{1,0:T(8,128)(2,1)} %constant.14.clone.y_low) | copy-start | bytes 393220
  33.5 0.9 %copy-start.7 = (bf16[256,256]{1,0:T(8,128)(2,1)S(1)}, bf16[256,256]{1,0:T(8,128)(2,1)}, u32[]{:S(2)}) copy-start(bf16[256,256]{1,0:T(8,128)(2,1)} %constant.13.clone.y_high) | copy-start | bytes 393220
  34.4 0.7 copy-start.10
  35.1 0.7 copy-start.12

commit v4 on v3

--- a/solution.py
+++ b/solution.py
@@ -26,11 +26,19 @@
 
 
 def spread_kernel(
-    owner_ref, cell_ref, fx_ref, fy_ref, mass_ref, live_ref,
+    owner_hbm, cell_hbm, fx_hbm, fy_hbm, mass_hbm, live_hbm,
     main_ref, rim_ref, total_ref,
+    owner_ref, cell_ref, fx_ref, fy_ref, mass_ref, live_ref, in_sem,
     grid_acc, rim_acc, lx_s, ly_s, fx_s, fy_s, w_s,
 ):
     tiles = cell_ref.shape[0]
+    sources = (owner_hbm, cell_hbm, fx_hbm, fy_hbm, mass_hbm, live_hbm)
+    homes = (owner_ref, cell_ref, fx_ref, fy_ref, mass_ref, live_ref)
+    arrivals = [
+        pltpu.make_async_copy(source, home, in_sem.at[k]) for k, (source, home) in enumerate(zip(sources, homes))
+    ]
+    for copy in arrivals:
+        copy.start()
     zero = jnp.zeros((8, TILE), jnp.float32)
 
     def clear(i, _):
@@ -46,6 +54,9 @@
         return 0
 
     lax.fori_loop(0, OWNERS, clear_rim, 0)
+
+    for copy in arrivals:
+        copy.wait()
 
     def prepare(i, _):
         rows = pl.ds(pl.multiple_of(i * 16, 16), 16)
@@ -80,7 +91,7 @@
         rim = lax.dot_general(wr, wx, NT, preferred_element_type=jnp.float32)
         return main, rim[:8]
 
-    unroll = 32
+    unroll = 64
 
     def add_tiles(i, _):
         results = [one_tile(i * unroll + k) for k in range(unroll)]
@@ -138,9 +149,16 @@
             jax.ShapeDtypeStruct((2, 16, 2, 8, TILE), jnp.float32),
             jax.ShapeDtypeStruct((8, TILE), jnp.float32),
         ),
-        in_specs=[pl.BlockSpec(memory_space=pltpu.SMEM)] + [vmem] * 5,
+        in_specs=[pl.BlockSpec(memory_space=pltpu.HBM)] * 6,
         out_specs=(vmem, vmem, vmem),
         scratch_shapes=[
+            pltpu.SMEM((1, tiles), jnp.int32),
+            pltpu.VMEM((tiles, TILE), jnp.int32),
+            pltpu.VMEM((tiles, TILE), jnp.bfloat16),
+            pltpu.VMEM((tiles, TILE), jnp.bfloat16),
+            pltpu.VMEM((tiles, TILE), jnp.bfloat16),
+            pltpu.VMEM((tiles, TILE), jnp.int32),
+            pltpu.SemaphoreType.DMA((6,)),
             pltpu.VMEM((PLANES, NX + 16, TILE), jnp.float32),
             pltpu.VMEM((OWNERS * PLANES, 8, TILE), jnp.float32),
             pltpu.VMEM((tiles, TILE), jnp.int32),
@@ -151,7 +169,7 @@
         ],
         compiler_params=pltpu.CompilerParams(vmem_limit_bytes=24 << 20),
         name="spread",
-    )(owners, cells, fx, fy, mass, live)
+    )(*(pltpu.with_memory_space_constraint(a, pltpu.HBM) for a in (owners, cells, fx, fy, mass, live)))
 
 
 COORDS = ("px_0", "px_1", "px_2")
@@ -244,14 +262,10 @@
 MESH = pl.DeviceIdType.MESH
 
 
-def place(index):
-    row = index // 8
-    return {"px_0": row // 8, "px_1": lax.rem(row // 2, 4), "px_2": lax.rem(row, 2), "py": lax.rem(index, 8)}
-
-
 def transform_kernel(
-    main_ref, rim_ref, total_ref, counts_ref, twist_y, y_high, y_low,
+    main_ref, rim_ref, total_ref, counts_hbm, twist_hbm, y_high_hbm, y_low_hbm,
     columns, begin_out,
+    counts_ref, twist_y, y_high, y_low, table_sem,
     main0, rim0, main1, rim1, main2, rim2, main3, rim3, main4, rim4,
     note, notes, pack, got, waves,
     note_send, note_recv, send, recv, py_send, py_recv, wave_send, wave_recv,
@@ -263,12 +277,25 @@
     barrier = pltpu.get_barrier_semaphore()
 
     def device(x, y, c):
-        return ((x * 4 + y) * 2 + c) * 8 + j
-
-    for k in range(1, OWNERS):
-        pl.semaphore_signal(barrier, inc=1, device_id=place(lax.rem(me + 8 * k, DEVICES)), device_id_type=MESH)
+        return {"px_0": x, "px_1": y, "px_2": c}
+
+    tables_in = [
+        pltpu.make_async_copy(table, spot, table_sem.at[k])
+        for k, (table, spot) in enumerate(
+            ((counts_hbm, counts_ref), (twist_hbm, twist_y), (y_high_hbm, y_high), (y_low_hbm, y_low))
+        )
+    ]
+    for copy in tables_in:
+        copy.start()
+    xs = [x] + [lax.rem(x + k, 4) for k in range(1, 4)]
+    ys = [y] + [lax.rem(y + k, 4) for k in range(1, 4)]
+    js = [j] + [lax.rem(j + k, 8) for k in range(1, 8)]
+    column = [(xs[a], ys[b], (c, 1 - c)[d]) for a in range(4) for b in range(4) for d in range(2)][1:]
+    for peer in column:
+        pl.semaphore_signal(barrier, inc=1, device_id=device(*peer), device_id_type=MESH)
     for k in range(1, 8):
-        pl.semaphore_signal(barrier, inc=1, device_id=place(i * 8 + lax.rem(j + k, 8)), device_id_type=MESH)
+        pl.semaphore_signal(barrier, inc=1, device_id={"py": js[k]}, device_id_type=MESH)
+    tables_in[0].wait()
     note[0:1, :] = counts_ref[0, :, 0:TILE].astype(jnp.float32)
     note[1:2, :] = counts_ref[0, :, TILE:].astype(jnp.float32)
     note[2:3, :] = jnp.sum(total_ref[...], axis=0, keepdims=True)
@@ -279,7 +306,7 @@
     def remote(src, dst, slot, where):
         copy = pltpu.make_async_remote_copy(
             src_ref=src, dst_ref=dst, send_sem=send.at[slot], recv_sem=recv.at[slot],
-            device_id=place(where), device_id_type=MESH,
+            device_id=where, device_id_type=MESH,
         )
         copy.start()
         return copy
@@ -310,15 +337,14 @@
     for k, (src, b0, *_) in chunks.items():
         pending[k] = [remote(src.at[:, :, 1 - c], b0, 7 * k, device(x, y, 1 - c))]
 
-    def note_copy(k):
-        peer = lax.rem(i + k, OWNERS)
+    def note_copy(peer, slot, source):
         return pltpu.make_async_remote_copy(
-            src_ref=note, dst_ref=notes.at[i], send_sem=note_send.at[peer], recv_sem=note_recv.at[i],
-            device_id=place(peer * 8 + j), device_id_type=MESH,
+            src_ref=note, dst_ref=notes.at[source], send_sem=note_send.at[slot], recv_sem=note_recv.at[source],
+            device_id=device(*peer), device_id_type=MESH,
         )
 
-    for k in range(1, OWNERS):
-        note_copy(k).start()
+    for k, peer in enumerate(column):
+        note_copy(peer, k, i).start()
     sent = []
 
     def arrive(k):
@@ -377,12 +403,8 @@
         block = b0.at[x, other] if first == "x" else b0.at[other, y]
         pending[k] = [remote(block, b4, 7 * k + 6, where)]
 
-    for k in range(1, OWNERS):
-        peer = lax.rem(i + k, OWNERS)
-        copy = pltpu.make_async_remote_copy(
-            src_ref=note, dst_ref=notes.at[peer], send_sem=note_send.at[peer], recv_sem=note_recv.at[peer],
-            device_id=place(peer * 8 + j), device_id_type=MESH,
-        )
+    for k, peer in enumerate(column):
+        copy = note_copy(peer, k, (peer[0] * 4 + peer[1]) * 2 + peer[2])
         copy.wait_send()
         copy.wait_recv()
     everyone = notes[0]
@@ -393,7 +415,7 @@
     def plane_copy(k, source):
         return pltpu.make_async_remote_copy(
             src_ref=pack.at[k], dst_ref=got.at[source], send_sem=py_send.at[k], recv_sem=py_recv.at[source],
-            device_id=place(i * 8 + k), device_id_type=MESH,
+            device_id={"py": k}, device_id_type=MESH,
         )
 
     for k, (src, b0, b1, b2, b3, b4, route) in chunks.items():
@@ -428,10 +450,12 @@
     begin_out[2:8, :] = jnp.zeros((6, TILE), jnp.float32)
 
     for k in range(1, 8):
-        peer = lax.rem(j + k, 8)
+        peer = js[k]
         plane_copy(peer, j).wait_send()
         plane_copy(peer, peer).wait_recv()
 
+    for copy in tables_in[1:]:
+        copy.wait()
     lane = lax.broadcasted_iota(jnp.int32, (RX, TILE), 1)
     rims = jnp.concatenate([got[s, 32:40, :] for s in range(8)])
     rims = pltpu.roll(rims, (TILE - 32 * (j % 4)) % TILE, 1)
@@ -463,17 +487,23 @@
 
     columns[j * 32 + i] = waves[me]
 
-    def hand_out(k, _):
-        for n in range(5):
-            peer = lax.rem(me + 5 * k + n + 1, DEVICES)
-            pltpu.make_async_remote_copy(
-                src_ref=waves.at[peer], dst_ref=columns.at[j * 32 + i],
-                send_sem=wave_send, recv_sem=wave_recv,
-                device_id=place(peer), device_id_type=MESH,
-            ).start()
+    def hand_out(row, place, n):
+        pltpu.make_async_remote_copy(
+            src_ref=waves.at[row * 8 + js[n]], dst_ref=columns.at[j * 32 + i],
+            send_sem=wave_send, recv_sem=wave_recv,
+            device_id={**place, "py": js[n]}, device_id_type=MESH,
+        ).start()
+
+    def hand_out_row(k, _):
+        row = lax.rem(i + k, OWNERS)
+        place = device(row // 8, lax.rem(row // 2, 4), lax.rem(row, 2))
+        for n in range(8):
+            hand_out(row, place, n)
         return 0
 
-    lax.fori_loop(0, (DEVICES - 1) // 5, hand_out, 0)
+    lax.fori_loop(1, OWNERS, hand_out_row, 0)
+    for n in range(1, 8):
+        hand_out(i, {}, n)
     for copy in sent:
         copy.wait_send()
     others = columns.at[pl.ds(0, DEVICES - 1)]
@@ -495,9 +525,14 @@
             jax.ShapeDtypeStruct((DEVICES, 2, TILE), f32),
             jax.ShapeDtypeStruct((8, TILE), f32),
         ),
-        in_specs=[vmem] * 7,
+        in_specs=[vmem] * 3 + [pl.BlockSpec(memory_space=pltpu.HBM)] * 4,
         out_specs=(vmem, vmem),
         scratch_shapes=[
+            pltpu.VMEM((1, 1, 2 * TILE), jnp.int32),
+            pltpu.VMEM((2, 8, TILE), f32),
+            pltpu.VMEM((2 * TILE, 2 * TILE), jnp.bfloat16),
+            pltpu.VMEM((2 * TILE, 2 * TILE), jnp.bfloat16),
+            dma((4,)),
             *both(4, 4), *both(2, 4), *both(4), *both(2), *both(),
             pltpu.VMEM((8, TILE), f32),
             pltpu.VMEM((OWNERS, 8, TILE), f32),
@@ -510,7 +545,7 @@
             collective_id=0, has_side_effects=True, vmem_limit_bytes=24 << 20
         ),
         name="transform",
-    )(main, rim, total, counts, *wave_tables)
+    )(main, rim, total, *(pltpu.with_memory_space_constraint(a, pltpu.HBM) for a in (counts, *wave_tables)))
 
 
 def finish_kernel(columns, begin_ref, x_both, x_low, twist_x, out_ref, start_ref):

time: 87.6 us -> 75.2 us (0.86)
  local copies, waits for them, and re-layouts: 8.56 us -> 0.02 us
  Pallas kernels: 77.9 us -> 74.6 us
    unnamed x26 -> x6, local copies, waits for them, and re-layouts: 8.56 us -> 0.02 us
    pallas_call x1, Pallas kernels: 50.2 us -> 48.4 us  [transform(): pl.pallas_call(transform_kernel, out_shape=(jax.ShapeDtypeStruct((DEVICES...]
    pallas_call x1, Pallas kernels: 26.5 us -> 24.9 us  [spread(): pl.pallas_call(spread_kernel, out_shape=(jax.ShapeDtypeStruct((PLANES, 16...]
where the time goes in v4:
time: 75.2 us; the launch traced here: 75.3 us
  Pallas kernels  74.6 us (99%)
    pallas_call x1, Pallas kernels, transform(): pl.pallas_call(transform_kernel, out_shape=(jax.ShapeDtypeStruct((DEVICES...  48.4 us
    pallas_call x1, Pallas kernels, spread(): pl.pallas_call(spread_kernel, out_shape=(jax.ShapeDtypeStruct((PLANES, 16...  24.9 us

profile of v4, /device:TPU:1, one launch (start us, length us, event | category | flops | bytes accessed | tf_op | source)
XLA Modules:
  0.0 75.3 jit_solution(16020052096403006743)
XLA Ops:
  0.6 0.0 copy-start.2
  0.6 0.0 copy-start.1
  0.7 0.0 copy-start
  0.7 24.9 %spread.1 = (f32[8,16,2,32,128]{4,3,2,1,0:T(8,128)S(1)}, f32[2,16,2,8,128]{4,3,2,1,0:T(8,128)S(1)}, f32[8,128]{1,0:T(8,128)S(1)}) custom-call(s32[1,640]{1,0:T(1,128)} %owner_hbm.1, s32[640,128]{1,0:T(8,128)} %bitcast.9, bf16[640,128]{1,0:T(8,128)(2,1)} %bitcast.11, bf16[640,128]{1,0:T(8,128)(2,1)} %bitcast.12, bf16[640,128]{1,0:T(8,128)(2,1)} %bitcast.13, ...), custom_call_target="tpu_custom_call" | custom-call | tf_op jit(solution)/shard_map/spread/pallas_call | solution.py:145
  25.5 48.4 %transform.1 = (f32[256,2,128]{2,1,0:T(2,128)S(1)}, f32[8,128]{1,0:T(8,128)S(1)}) custom-call(f32[8,4,4,2,32,128]{5,4,3,2,1,0:T(8,128)S(1)} %bitcast.7, f32[2,4,4,2,8,128]{5,4,3,2,1,0:T(8,128)S(1)} %bitcast.8, f32[8,128]{1,0:T(8,128)S(1)} %get-tuple-element.9.total_ref, s32[1,1,256]{2,1,0:T(1,128)} %counts_hbm.1, f32[2,8,128]{2,1,0:T(8,128)} %constant.12.clone.twist_hbm, ...), custom_call_target="tpu_custom_call" | custom-call | tf_op jit(solution)/shard_map/transform/pallas_call | solution.py:522
  74.0 0.0 copy-done.2
  74.0 0.0 copy-done.1
  74.0 0.0 copy-done
  74.0 1.2 %finish.1 = (f32[2,8,4,1024]{3,2,1,0:T(4,128)}, s32[1,1,256]{2,1,0:T(1,128)}) custom-call(f32[256,2,128]{2,1,0:T(2,128)S(1)} %get-tuple-element.10.columns, f32[8,128]{1,0:T(8,128)S(1)} %get-tuple-element.11.begin_ref, bf16[256,512]{1,0:T(8,128)(2,1)S(1)} %copy-done, bf16[128,512]{1,0:T(8,128)(2,1)S(1)} %copy-done.1, f32[2,32,128]{2,1,0:T(8,128)S(1)} %copy-done.2), custom_call_target="tpu_custom_call" | custom-call | tf_op jit(solution)/shard_map/finish/pallas_call | solution.py:583
Async XLA Ops:
  0.6 73.4 %copy-start.2 = (f32[2,32,128]{2,1,0:T(8,128)S(1)}, f32[2,32,128]{2,1,0:T(8,128)}, u32[]{:S(2)}) copy-start(f32[2,32,128]{2,1,0:T(8,128)} %constant.17.clone.twist_x) | copy-start | bytes 98308
  0.6 73.4 %copy-start.1 = (bf16[128,512]{1,0:T(8,128)(2,1)S(1)}, bf16[128,512]{1,0:T(8,128)(2,1)}, u32[]{:S(2)}) copy-start(bf16[128,512]{1,0:T(8,128)(2,1)} %constant.16.clone.x_low) | copy-start | bytes 393220
  0.7 73.4 %copy-start = (bf16[256,512]{1,0:T(8,128)(2,1)S(1)}, bf16[256,512]{1,0:T(8,128)(2,1)}, u32[]{:S(2)}) copy-start(bf16[256,512]{1,0:T(8,128)(2,1)} %constant.15.clone.x_both) | copy-start | bytes 786436
